TPU v7x, 32 devices: a whole 2x2x4 slice. The times are simulated.
32 devices in a mesh: batch: 8 (over y, x, core), heads: 4 (over z).
Axes of the slice: x: 2, y: 2, z: 4, core: 2. Of those that a mesh axis runs over, the one named last changes fastest.
Arguments:
- tokens: bfloat16 [24576, 768], P('batch'), may hold values from -5 to 5
- qkv_weight: bfloat16 [768, 3, 768], P(None, None, 'heads'), may hold values from -0.21875 to 0.21875
- qv_bias: float32 [2, 768], replicated, may hold values from -3 to 3
- conv_weight: float32 [12, 33], replicated, may hold values from -0.875 to 0.875
- out_weight: bfloat16 [768, 768], P('heads'), may hold values from -0.21875 to 0.21875
- out_bias: float32 [768], replicated, may hold values from -1.75 to 1.75
- norm1_gain: float32 [768], replicated, may hold values from 0.5 to 1.5
- norm1_bias: float32 [768], replicated, may hold values from -1.75 to 1.75
- ffn_in_weight: bfloat16 [768, 3072], P(None, ('batch', 'heads')), may hold values from -0.21875 to 0.21875
- ffn_in_bias: bfloat16 [3072], P(('batch', 'heads')), may hold values from -3 to 3
- ffn_out_weight: bfloat16 [3072, 768], P(('batch', 'heads')), may hold values from -0.109375 to 0.109375
- ffn_out_bias: float32 [768], replicated, may hold values from -1.75 to 1.75
- norm2_gain: float32 [768], replicated, may hold values from 0.5 to 1.5
- norm2_bias: float32 [768], replicated, may hold values from -1.75 to 1.75
- cotangent: bfloat16 [24576, 768], P(('batch', 'heads')), may hold values from -12 to 12
- seq_lengths: int32 [24], P('batch'), may hold values from 0 to 3072, as said below
- segment_ids: int32 [24576], P('batch'), may hold values from 0 to 3, as said below
- landmark_bounds: int32 [24, 64], P('batch'), may hold values from 0 to 3024, as said below
Outputs:
- out: bfloat16 [24576, 768], P(('batch', 'heads'))
- input_grad: float32 [24576, 768], P(('batch', 'heads'))
- qkv_weight_grad: float32 [768, 3, 768], P('batch', None, 'heads')
- qv_bias_grad: float32 [2, 768], P(None, 'heads')
- conv_grad: float32 [12, 33], P('heads')
- out_weight_grad: float32 [768, 768], P('heads', 'batch')
- ffn_in_grad: float32 [768, 3072], P(None, ('batch', 'heads'))
- ffn_in_bias_grad: float32 [3072], P(('batch', 'heads'))
- ffn_out_grad: float32 [3072, 768], P(('batch', 'heads'))
- vector_grads: float32 [6, 768], P(None, ('batch', 'heads'))
- condition: float32 [], replicated
Inputs may be any that keep to these rules, and one draw needn't show every extreme that they name: `seq_lengths`: each index of batch holds 3 slots: sequences of 1024 to 3072 tokens first, then empty slots of length 0; the lengths of one index sum to at most 3072; at least one index holds a single sequence of 3072 tokens. `segment_ids`: the live tokens of an index of batch lie in order of slot from its first token slot on, each slot's tokens contiguous; the remaining token slots carry 3. landmark_bounds[s, j] = (j times the length of slot s) // 64.
All inputs are finite; a program needn't handle non-finite values.
Results may differ from a plain program's by a relative error of at most 0.013.
Values may be sent and summed in bfloat16 or wider, within the bound.
A program may use at most 448 MiB of HBM per device.

v0:
```python
from functools import partial

import jax
import jax.numpy as jnp
from jax import lax
from jax.experimental import pallas as pl
from jax.experimental.pallas import tpu as pltpu
from jax.sharding import PartitionSpec as P

HEAD_DIM = 64
PINV_ITERS = 6
TILE = 512
SUB = 128

f32 = jnp.float32
low = jnp.bfloat16
mask_fill = -1000000000.0


def split(x):
    high = x.astype(low)
    return high, (x - high.astype(f32)).astype(low)


def mul(a, b):
    return lax.dot_general(a, b, (((1,), (0,)), ((), ())), preferred_element_type=f32)


def mul_t(a, b):
    return lax.dot_general(a, b, (((1,), (1,)), ((), ())), preferred_element_type=f32)


def wide(form, left, right):
    left_high, left_low = split(left)
    right_high, right_low = split(right)
    return form(left_high, right_high) + (
        form(left_high, right_low) + form(left_low, right_high)
    )


def block_grid(rows, cols):
    row_block = lax.broadcasted_iota(jnp.int32, (rows, cols), 0) // HEAD_DIM
    col_block = lax.broadcasted_iota(jnp.int32, (rows, cols), 1) // HEAD_DIM
    return row_block == col_block


def spread(x, blocks):
    count = blocks.shape[0] // x.shape[0]
    return jnp.where(blocks, jnp.concatenate([x] * count, axis=0), jnp.zeros_like(x[:1, :1]))


def fold(x, blocks):
    kept = jnp.where(blocks, x, jnp.zeros_like(x[:1, :1]))
    rows = HEAD_DIM
    out = kept[:rows]
    for n in range(1, x.shape[0] // rows):
        out = out + kept[n * rows : (n + 1) * rows]
    return out


def pack_mul(left, right, blocks):
    left_high, left_low = split(left)
    right_high, right_low = split(right)
    right_high, right_low = spread_low(right_high, blocks), spread_low(right_low, blocks)
    return mul(left_high, right_high) + (mul(left_high, right_low) + mul(left_low, right_high))


def pack_mul_t(left, right, blocks):
    left_high, left_low = split(left)
    right_high, right_low = split(right)
    right_high, right_low = spread_low(right_high, blocks), spread_low(right_low, blocks)
    return mul_t(left_high, right_high) + (mul_t(left_high, right_low) + mul_t(left_low, right_high))


def spread_low(x, blocks):
    return spread(x.astype(f32), blocks).astype(low)


def slot_bounds(len_ref, s, slots):
    start = jnp.int32(0)
    for n in range(slots):
        start = start + jnp.where(n < s, len_ref[n], 0)
    return start, start + len_ref[s]


def eye_pack(width):
    row = lax.broadcasted_iota(jnp.int32, (HEAD_DIM, width), 0)
    col = lax.broadcasted_iota(jnp.int32, (HEAD_DIM, width), 1) % HEAD_DIM
    return jnp.where(row == col, 1.0, 0.0).astype(f32)


def lane_mask(start, end, at, width):
    tok = at + lax.broadcasted_iota(jnp.int32, (1, width), 1)
    return (tok >= start) & (tok < end)


def band(taps_row, width):
    row = lax.broadcasted_iota(jnp.int32, (SUB, 3 * SUB), 0)
    col = lax.broadcasted_iota(jnp.int32, (SUB, 3 * SUB), 1)
    off = col - row - (SUB - width // 2)
    out = jnp.zeros((SUB, 3 * SUB), f32)
    for n in range(width):
        out = jnp.where(off == n, taps_row[:, n : n + 1], out)
    return out


def slot_marks(len_ref, at, slots, marks, width):
    rows = slots * marks
    row = lax.broadcasted_iota(jnp.int32, (rows, 1), 0)
    slot = row // marks
    mark = row % marks
    start = jnp.zeros((rows, 1), jnp.int32)
    length = jnp.zeros((rows, 1), jnp.int32)
    for n in range(slots):
        start = start + jnp.where(slot > n, len_ref[n], 0)
        length = jnp.where(slot == n, len_ref[n], length)
    lower = start + (mark * length) // marks
    upper = start + ((mark + 1) * length) // marks
    inv_count = 1.0 / jnp.maximum((upper - lower).astype(f32), 1.0)
    tok = at + lax.broadcasted_iota(jnp.int32, (rows, width), 1)
    member = jnp.where((tok >= lower) & (tok < upper), 1.0, 0.0)
    return member, inv_count


def mix_forward_kernel(
    slots, marks, taps,
    len_ref, tok_ref, weight_ref, bias_ref, conv_ref,
    qkv_ref, first_ref, last_ref, mixed_ref, mark_ref, value_ref, inner_ref,
    denom_ref, middle_ref, steps_ref, inverse_ref, bound_ref,
    vpad, scores, vsum, bias_col, conv_own,
):
    step = pl.program_id(0)
    width = first_ref.shape[0]
    heads = width // HEAD_DIM
    tok_count = qkv_ref.shape[1]
    tiles = tok_count // TILE
    packed = slots * marks
    at = pl.multiple_of(step * TILE, TILE)

    @pl.when(step == 0)
    def _():
        z = lax.axis_index("heads")
        own_taps(conv_own, conv_ref, z)
        columns = jnp.transpose(jnp.concatenate([bias_ref[...], bias_ref[...]], axis=0))
        bias_col[: bias_ref.shape[1], :] = columns
        mark_ref[...] = jnp.zeros_like(mark_ref)
        vsum[...] = jnp.zeros_like(vsum)
        vpad[:, :SUB] = jnp.zeros((width, SUB), low)
        vpad[:, tok_count + SUB :] = jnp.zeros((width, SUB), low)

    at_head = pl.ds(pl.multiple_of(lax.axis_index("heads") * width, HEAD_DIM), width)
    rows = mul_t(weight_ref[...], tok_ref[...])
    rows = jnp.concatenate(
        [
            rows[:width] + bias_col[at_head, 0:1],
            rows[width : 2 * width],
            rows[2 * width :] + bias_col[at_head, 1:2],
        ],
        axis=0,
    ).astype(low)
    qkv_ref[:, pl.ds(at, TILE)] = rows
    vpad[:, pl.ds(pl.multiple_of(at + SUB, SUB), TILE)] = rows[2 * width :]
    member, inv_count = slot_marks(len_ref, at, slots, marks, TILE)
    mark_ref[...] += mul_t(member.astype(low), rows[: 2 * width])
    vsum[...] += mul_t(jnp.ones((8, TILE), low), rows[2 * width :])
    first_ref[:, pl.ds(at, TILE)] = jnp.zeros((width, TILE), low)
    last_ref[:, pl.ds(at, TILE)] = jnp.zeros((width, TILE), low)
    mixed_ref[:, pl.ds(at, TILE)] = jnp.zeros((width, TILE), low)

    @pl.when(step == tiles - 1)
    def _():
        mark_ref[...] = mark_ref[...] * inv_count
        head_blocks = block_grid(width, width)
        slot_blocks = block_grid(packed, packed)
        eye = eye_pack(packed)
        scale = HEAD_DIM ** -0.5

        middles, inverses_t, products = [], [], []
        bound_total = jnp.zeros((1, 1), f32)
        lane_slot = lax.broadcasted_iota(jnp.int32, (1, packed), 1) // marks
        for h in range(heads):
            q_marks = mark_ref[:, h * HEAD_DIM : (h + 1) * HEAD_DIM]
            k_marks = mark_ref[:, width + h * HEAD_DIM : width + (h + 1) * HEAD_DIM]
            sim = wide(mul_t, q_marks, k_marks) * scale
            sim = jnp.where(slot_blocks, sim, -1e30)
            sim = jnp.exp(sim - jnp.max(sim, axis=1, keepdims=True))
            sim = sim / jnp.sum(sim, axis=1, keepdims=True)
            middle = fold(sim, slot_blocks)
            col_sums = jnp.sum(middle, axis=0, keepdims=True)
            bound = jnp.zeros((1, packed), f32)
            for s in range(slots):
                top = jnp.max(jnp.where(lane_slot == s, col_sums, 0.0), axis=1, keepdims=True)
                bound = jnp.where(lane_slot == s, top, bound)
                bound_total += jnp.where(len_ref[s] > 0, top, 0.0)
            middle_ref[h] = middle
            middles.append(middle)
            inverses_t.append(middle / bound)
            products.append(pack_mul_t(middle, middle, slot_blocks) / bound)
        bound_ref[...] = jnp.broadcast_to(bound_total, bound_ref.shape)

        def newton(n, carry):
            out = []
            for h in range(heads):
                inverse_t, product = carry[h]
                square = pack_mul(product, product, slot_blocks)
                cube = pack_mul(product, square, slot_blocks)
                fourth = pack_mul(square, square, slot_blocks)
                second = 15.0 * eye - 7.0 * product + square
                third = 13.0 * eye - 15.0 * product + 7.0 * square - cube
                steps_ref[n, 0, h] = product
                steps_ref[n, 1, h] = second
                steps_ref[n, 2, h] = third
                steps_ref[n, 3, h] = inverse_t
                out.append(
                    (
                        0.25 * pack_mul(third, inverse_t, slot_blocks),
                        0.25 * (13.0 * product - 15.0 * square + 7.0 * cube - fourth),
                    )
                )
            return tuple(out)

        final = lax.fori_loop(0, PINV_ITERS, newton, tuple(zip(inverses_t, products)))
        for h in range(heads):
            inverse_ref[h] = final[h][0]

        def one_slot(s, _):
            start, end = slot_bounds(len_ref, s, slots)
            lo, hi = start // TILE, (end + TILE - 1) // TILE
            hi = jnp.where(end > start, hi, lo)
            own = mark_ref[pl.ds(pl.multiple_of(s * marks, marks), marks), :] * scale
            q_block = spread(own[:, :width], head_blocks).astype(low)
            k_block = spread(own[:, width:], head_blocks).astype(low)

            def score_tile(n, top):
                t = pl.multiple_of(n * TILE, TILE)
                mask = lane_mask(start, end, t, TILE)
                sim = mul(k_block, qkv_ref[:width, pl.ds(t, TILE)])
                sim = sim.reshape(heads, marks, TILE)
                sim = jnp.exp(sim - jnp.max(sim, axis=1, keepdims=True))
                sim = sim / jnp.sum(sim, axis=1, keepdims=True)
                sim = sim.reshape(width, TILE)
                old = first_ref[:, pl.ds(t, TILE)].astype(f32)
                first_ref[:, pl.ds(t, TILE)] = jnp.where(mask, sim, old).astype(low)
                sim = mul(q_block, qkv_ref[width : 2 * width, pl.ds(t, TILE)])
                sim = jnp.where(mask, sim, mask_fill)
                scores[:, pl.ds(t, TILE)] = sim
                for c in range(TILE // SUB):
                    top = jnp.maximum(top, sim[:, c * SUB : (c + 1) * SUB])
                return top

            top = lax.fori_loop(lo, hi, score_tile, jnp.full((width, SUB), mask_fill, f32))
            top = jnp.max(top, axis=1, keepdims=True)

            def value_tile(n, carry):
                denom, total = carry
                t = pl.multiple_of(n * TILE, TILE)
                mask = lane_mask(start, end, t, TILE)
                part = jnp.exp(scores[:, pl.ds(t, TILE)] - top)
                old = last_ref[:, pl.ds(t, TILE)].astype(f32)
                last_ref[:, pl.ds(t, TILE)] = jnp.where(mask, part, old).astype(low)
                total = total + mul_t(part.astype(low), qkv_ref[2 * width :, pl.ds(t, TILE)])
                for c in range(TILE // SUB):
                    denom = denom + part[:, c * SUB : (c + 1) * SUB]
                return denom, total

            denom, total = lax.fori_loop(
                lo, hi, value_tile,
                (jnp.zeros((width, SUB), f32), jnp.zeros((width, width), f32)),
            )
            denom = jnp.sum(denom, axis=1, keepdims=True)
            inv = 1.0 / jnp.where(denom > 0.0, denom, 1.0)
            denom_ref[s] = inv
            values = fold(total * inv, head_blocks)
            values = jnp.where(end > start, values, vsum[:1] / tok_count)
            value_ref[pl.ds(pl.multiple_of(s * marks, marks), marks), :] = values
            return 0

        lax.fori_loop(0, slots, one_slot, 0)

        lane_head = lax.broadcasted_iota(jnp.int32, (1, width), 1) // HEAD_DIM
        inner = jnp.zeros((packed, width), f32)
        for h in range(heads):
            inverse = pack_mul_t(eye, final[h][0], slot_blocks)
            own_values = jnp.where(lane_head == h, value_ref[...], 0.0)
            inner = inner + wide(mul, spread(inverse, slot_blocks), own_values)
        inner_ref[...] = inner

        bands = [band(conv_own[h : h + 1, :], taps).astype(low) for h in range(heads)]

        def out_slot(s, _):
            start, end = slot_bounds(len_ref, s, slots)
            lo, hi = start // TILE, (end + TILE - 1) // TILE
            hi = jnp.where(end > start, hi, lo)
            own = inner_ref[pl.ds(pl.multiple_of(s * marks, marks), marks), :]
            a_block = jnp.transpose(spread(own, head_blocks)).astype(low)

            def out_tile(n, _):
                t = pl.multiple_of(n * TILE, TILE)
                mask = lane_mask(start, end, t, TILE)
                rows = mul(a_block, first_ref[:, pl.ds(t, TILE)])
                rows = rows + convolve(vpad, bands, start, end, t, heads)
                old = mixed_ref[:, pl.ds(t, TILE)].astype(f32)
                mixed_ref[:, pl.ds(t, TILE)] = jnp.where(mask, rows, old).astype(low)
                return 0

            return lax.fori_loop(lo, hi, out_tile, 0)

        lax.fori_loop(0, slots, out_slot, 0)


def own_taps(own_ref, all_ref, z):
    heads = own_ref.shape[0]
    for n in range(all_ref.shape[0] // heads):

        @pl.when(z == n)
        def _():
            own_ref[...] = all_ref[n * heads : (n + 1) * heads, :]


def windows(padded, start, end, t):
    full = padded[:, pl.ds(t, TILE + 2 * SUB)]
    keep = lane_mask(start, end, t - SUB, TILE + 2 * SUB)
    return jnp.where(keep, full.astype(f32), 0.0).astype(low)


def convolve(padded, bands, start, end, t, heads):
    full = windows(padded, start, end, t)
    out = []
    count = TILE // SUB
    for h in range(heads):
        own = full[h * HEAD_DIM : (h + 1) * HEAD_DIM]
        stack = jnp.concatenate(
            [own[:, c * SUB : (c + 3) * SUB] for c in range(count)], axis=0
        )
        res = mul_t(stack, bands[h])
        out.append(
            jnp.concatenate(
                [res[c * HEAD_DIM : (c + 1) * HEAD_DIM] for c in range(count)], axis=1
            )
        )
    return jnp.concatenate(out, axis=0)


def mix_backward_kernel(
    slots, marks, taps,
    len_ref, grad_ref, qkv_ref, first_ref, last_ref, mark_ref, value_ref, inner_ref,
    denom_ref, middle_ref, steps_ref, inverse_ref, conv_ref,
    out_ref, bias_ref, conv_out_ref,
    gpad, vpad, ds_first, ds_last, conv_grad, d_inner, d_k, d_q, d_value, conv_own,
):
    width = first_ref.shape[0]
    heads = width // HEAD_DIM
    tok_count = qkv_ref.shape[1]
    packed = slots * marks
    scale = HEAD_DIM ** -0.5
    head_blocks = block_grid(width, width)
    slot_blocks = block_grid(packed, packed)
    eye = eye_pack(packed)
    count = TILE // SUB

    for padded, source in ((gpad, grad_ref[...]), (vpad, qkv_ref[2 * width :, :])):
        padded[:, :SUB] = jnp.zeros((width, SUB), low)
        padded[:, tok_count + SUB :] = jnp.zeros((width, SUB), low)
        padded[:, SUB : tok_count + SUB] = source
    out_ref[...] = jnp.zeros_like(out_ref)
    ds_first[...] = jnp.zeros_like(ds_first)
    ds_last[...] = jnp.zeros_like(ds_last)
    conv_grad[...] = jnp.zeros_like(conv_grad)

    own_taps(conv_own, conv_ref, lax.axis_index("heads"))

    def reach(s):
        start, end = slot_bounds(len_ref, s, slots)
        lo, hi = start // TILE, (end + TILE - 1) // TILE
        return start, end, lo, jnp.where(end > start, hi, lo)

    def own_rows(s):
        return pl.ds(pl.multiple_of(s * marks, marks), marks)

    def first_slot(s, _):
        start, end, lo, hi = reach(s)
        a_block = spread(inner_ref[own_rows(s), :], head_blocks).astype(low)

        def tile(n, carry):
            inner_total, key_total = carry
            t = pl.multiple_of(n * TILE, TILE)
            mask = lane_mask(start, end, t, TILE)
            own_grad = grad_ref[:, pl.ds(t, TILE)]
            kernel_rows = jnp.where(mask, first_ref[:, pl.ds(t, TILE)].astype(f32), 0.0)
            d_kernel = mul(a_block, own_grad)
            prod = (kernel_rows * d_kernel).reshape(heads, marks, TILE)
            row_sum = jnp.sum(prod, axis=1, keepdims=True)
            d_sim = prod - kernel_rows.reshape(heads, marks, TILE) * row_sum
            d_sim = d_sim.reshape(width, TILE)
            d_sim_low = d_sim.astype(low)
            old = ds_first[:, pl.ds(t, TILE)].astype(f32)
            ds_first[:, pl.ds(t, TILE)] = jnp.where(mask, d_sim, old).astype(low)
            inner_total = inner_total + mul_t(kernel_rows.astype(low), own_grad)
            key_total = key_total + mul_t(d_sim_low, qkv_ref[:width, pl.ds(t, TILE)])
            full = windows(vpad, start, end, t)
            grad_own = jnp.where(mask, own_grad.astype(f32), 0.0).astype(low)
            for h in range(heads):
                sel = slice(h * HEAD_DIM, (h + 1) * HEAD_DIM)
                left = jnp.concatenate(
                    [grad_own[sel, c * SUB : (c + 1) * SUB] for c in range(count)], axis=0
                )
                right = jnp.concatenate(
                    [full[sel, c * SUB : (c + 3) * SUB] for c in range(count)], axis=0
                )
                conv_grad[h] += lax.dot_general(
                    left, right, (((0,), (0,)), ((), ())), preferred_element_type=f32
                )
            return inner_total, key_total

        zero = jnp.zeros((width, width), f32)
        inner_total, key_total = lax.fori_loop(lo, hi, tile, (zero, zero))
        d_inner[own_rows(s), :] = fold(inner_total, head_blocks)
        d_k[own_rows(s), :] = fold(key_total, head_blocks) * scale
        return 0

    lax.fori_loop(0, slots, first_slot, 0)

    row = lax.broadcasted_iota(jnp.int32, (SUB, 3 * SUB), 0)
    col = lax.broadcasted_iota(jnp.int32, (SUB, 3 * SUB), 1)
    off = col - row - (SUB - taps // 2)
    tap_lane = lax.broadcasted_iota(jnp.int32, (1, SUB), 1)
    for h in range(heads):
        found = jnp.zeros((1, SUB), f32)
        square = conv_grad[h]
        for n in range(taps):
            part = jnp.sum(jnp.where(off == n, square, 0.0), axis=0, keepdims=True)
            part = jnp.sum(part, axis=1, keepdims=True)
            found = jnp.where(tap_lane == n, part, found)
        conv_out_ref[h : h + 1, :] = found

    lane_head = lax.broadcasted_iota(jnp.int32, (1, width), 1) // HEAD_DIM
    value_total = jnp.zeros((packed, width), f32)
    d_inverses = []
    for h in range(heads):
        own = jnp.where(lane_head == h, d_inner[...], 0.0)
        value_total = value_total + wide(mul, spread(inverse_ref[h], slot_blocks), own)
        d_inverses.append(fold(wide(mul_t, own, value_ref[...]), slot_blocks))
    d_value[...] = value_total

    middles_t = [pack_mul_t(eye, middle_ref[h], slot_blocks) for h in range(heads)]

    def newton(k, carry):
        n = PINV_ITERS - 1 - k
        out = []
        for h in range(heads):
            d_inverse, d_middle = carry[h]
            product = steps_ref[n, 0, h]
            second = steps_ref[n, 1, h]
            third = steps_ref[n, 2, h]
            inverse_t = steps_ref[n, 3, h]
            middle_t = middles_t[h]
            d_third = 0.25 * pack_mul(inverse_t, d_inverse, slot_blocks)
            d_second = -pack_mul(product, d_third, slot_blocks)
            d_first = -pack_mul(product, d_second, slot_blocks)
            d_product = (
                -pack_mul(d_third, second, slot_blocks)
                - pack_mul(d_second, 7.0 * eye - product, slot_blocks)
                - d_first
            )
            d_middle = d_middle + pack_mul(d_product, inverse_t, slot_blocks)
            d_inverse = 0.25 * pack_mul(d_inverse, third, slot_blocks) + pack_mul(
                middle_t, d_product, slot_blocks
            )
            out.append((d_inverse, d_middle))
        return tuple(out)

    zero = jnp.zeros((HEAD_DIM, packed), f32)
    final = lax.fori_loop(0, PINV_ITERS, newton, tuple((x, zero) for x in d_inverses))
    lane_slot = lax.broadcasted_iota(jnp.int32, (1, packed), 1) // marks
    dq_total = jnp.zeros((packed, width), f32)
    dk_total = jnp.zeros((packed, width), f32)
    for h in range(heads):
        d_inverse, d_middle = final[h]
        middle = middle_ref[h]
        first_t = steps_ref[0, 3, h]
        d_inverse_t = pack_mul_t(eye, d_inverse, slot_blocks)
        col_sums = jnp.sum(middle, axis=0, keepdims=True)
        share = jnp.sum(d_inverse_t * first_t, axis=0, keepdims=True)
        bound = jnp.zeros((1, packed), f32)
        d_bound = jnp.zeros((1, packed), f32)
        hits = jnp.zeros((1, packed), f32)
        for s in range(slots):
            mine = lane_slot == s
            top = jnp.max(jnp.where(mine, col_sums, 0.0), axis=1, keepdims=True)
            total = jnp.sum(jnp.where(mine, share, 0.0), axis=1, keepdims=True)
            number = jnp.sum(
                jnp.where(mine & (col_sums == top), 1.0, 0.0), axis=1, keepdims=True
            )
            bound = jnp.where(mine, top, bound)
            d_bound = jnp.where(mine, -total / top, d_bound)
            hits = jnp.where(mine, number, hits)
        d_middle = d_middle + d_inverse_t / bound
        d_middle = d_middle + jnp.where(col_sums == bound, d_bound / hits, 0.0)
        prod = spread(middle * d_middle, slot_blocks)
        d_sim = prod - spread(middle, slot_blocks) * jnp.sum(prod, axis=1, keepdims=True)
        d_sim = d_sim * scale
        own = lane_head == h
        q_marks = jnp.where(own, mark_ref[:, :width], 0.0)
        k_marks = jnp.where(own, mark_ref[:, width:], 0.0)
        dq_total = dq_total + wide(mul, d_sim, k_marks)
        dk_total = dk_total + wide(mul, jnp.transpose(d_sim), q_marks)
    d_q[...] = dq_total
    d_k[...] += dk_total

    flipped = []
    for h in range(heads):
        flipped.append(
            band(
                jnp.concatenate(
                    [conv_own[h : h + 1, n : n + 1] for n in reversed(range(taps))], axis=1
                ),
                taps,
            ).astype(low)
        )

    def last_slot(s, _):
        start, end, lo, hi = reach(s)
        inv = denom_ref[s]
        own_d = d_value[own_rows(s), :]
        own_v = value_ref[own_rows(s), :]
        d_block = spread(own_d, head_blocks)
        row_sum = jnp.sum(
            d_block * jnp.concatenate([own_v] * heads, axis=0), axis=1, keepdims=True
        )
        row_sum = row_sum * inv
        d_block = d_block * inv
        d_block_t = jnp.transpose(d_block).astype(low)
        d_block = d_block.astype(low)

        def tile(n, query_total):
            t = pl.multiple_of(n * TILE, TILE)
            mask = lane_mask(start, end, t, TILE)
            kernel_rows = jnp.where(mask, last_ref[:, pl.ds(t, TILE)].astype(f32), 0.0)
            v_rows = qkv_ref[2 * width :, pl.ds(t, TILE)]
            d_sim = kernel_rows * (mul(d_block, v_rows) - row_sum)
            d_low = d_sim.astype(low)
            old = ds_last[:, pl.ds(t, TILE)].astype(f32)
            ds_last[:, pl.ds(t, TILE)] = jnp.where(mask, d_sim, old).astype(low)
            dv = mul(d_block_t, kernel_rows.astype(low))
            dv = dv + convolve(gpad, flipped, start, end, t, heads)
            old = out_ref[2 * width :, pl.ds(t, TILE)].astype(f32)
            out_ref[2 * width :, pl.ds(t, TILE)] = jnp.where(mask, dv, old).astype(low)
            return query_total + mul_t(d_low, qkv_ref[width : 2 * width, pl.ds(t, TILE)])

        query_total = lax.fori_loop(lo, hi, tile, jnp.zeros((width, width), f32))
        d_q[own_rows(s), :] += fold(query_total, head_blocks) * scale
        return 0

    lax.fori_loop(0, slots, last_slot, 0)

    inv_count = slot_marks(len_ref, 0, slots, marks, SUB)[1]
    d_q[...] = d_q[...] * inv_count
    d_k[...] = d_k[...] * inv_count

    def final_slot(s, _):
        start, end, lo, hi = reach(s)
        length = end - start
        own = mark_ref[own_rows(s), :] * scale

        def left(block, d_mark):
            wide_rows = jnp.concatenate([spread(block, head_blocks), d_mark], axis=0)
            return jnp.transpose(wide_rows).astype(low)

        q_left = left(own[:, width:], d_q[own_rows(s), :])
        k_left = left(own[:, :width], d_k[own_rows(s), :])
        mark = lax.broadcasted_iota(jnp.int32, (marks, 1), 0)
        lower = start + (mark * length) // marks
        upper = start + ((mark + 1) * length) // marks

        def tile(n, _):
            t = pl.multiple_of(n * TILE, TILE)
            mask = lane_mask(start, end, t, TILE)
            tok = t + lax.broadcasted_iota(jnp.int32, (marks, TILE), 1)
            member = jnp.where((tok >= lower) & (tok < upper), 1.0, 0.0).astype(low)
            for at, lhs, source in ((0, q_left, ds_first), (width, k_left, ds_last)):
                rhs = jnp.concatenate([source[:, pl.ds(t, TILE)], member], axis=0)
                rows = mul(lhs, rhs)
                old = out_ref[at : at + width, pl.ds(t, TILE)].astype(f32)
                out_ref[at : at + width, pl.ds(t, TILE)] = jnp.where(mask, rows, old).astype(low)
            return 0

        return lax.fori_loop(lo, hi, tile, 0)

    lax.fori_loop(0, slots, final_slot, 0)

    def bias_tile(n, carry):
        t = pl.multiple_of(n * TILE, TILE)
        q_sum, v_sum = carry
        q_rows = out_ref[:width, pl.ds(t, TILE)].astype(f32)
        v_rows = out_ref[2 * width :, pl.ds(t, TILE)].astype(f32)
        for c in range(count):
            q_sum = q_sum + q_rows[:, c * SUB : (c + 1) * SUB]
            v_sum = v_sum + v_rows[:, c * SUB : (c + 1) * SUB]
        return q_sum, v_sum

    zero = jnp.zeros((width, SUB), f32)
    q_sum, v_sum = lax.fori_loop(0, tok_count // TILE, bias_tile, (zero, zero))
    bias_ref[...] = jnp.zeros_like(bias_ref)
    bias_ref[0:1, :] = jnp.sum(jnp.transpose(q_sum), axis=0, keepdims=True)
    bias_ref[1:2, :] = jnp.sum(jnp.transpose(v_sum), axis=0, keepdims=True)


def mix_forward(seq_lengths, tokens, weight_t, bias, conv, slots, marks):
    tok_count, model = tokens.shape
    width = weight_t.shape[0] // 3
    heads = width // HEAD_DIM
    packed = slots * marks
    taps = conv.shape[1]
    whole = lambda *shape: pl.BlockSpec(shape, lambda i, lens: (0,) * len(shape))
    shapes = [
        ((3 * width, tok_count), low),
        ((width, tok_count), low),
        ((width, tok_count), low),
        ((width, tok_count), low),
        ((packed, 2 * width), f32),
        ((packed, width), f32),
        ((packed, width), f32),
        ((slots, width, 1), f32),
        ((heads, HEAD_DIM, packed), f32),
        ((PINV_ITERS, 4, heads, HEAD_DIM, packed), f32),
        ((heads, HEAD_DIM, packed), f32),
        ((8, 128), f32),
    ]
    return pl.pallas_call(
        partial(mix_forward_kernel, slots, marks, taps),
        out_shape=[jax.ShapeDtypeStruct(s, t) for s, t in shapes],
        grid_spec=pltpu.PrefetchScalarGridSpec(
            num_scalar_prefetch=1,
            grid=(tok_count // TILE,),
            in_specs=[
                pl.BlockSpec((TILE, model), lambda i, lens: (i, 0)),
                whole(3 * width, model),
                whole(*bias.shape),
                whole(*conv.shape),
            ],
            out_specs=[whole(*s) for s, _ in shapes],
            scratch_shapes=[
                pltpu.VMEM((width, tok_count + 2 * SUB), low),
                pltpu.VMEM((width, tok_count), f32),
                pltpu.VMEM((8, width), f32),
                pltpu.VMEM((bias.shape[1], 2 * bias.shape[0]), f32),
                pltpu.VMEM((heads, taps), f32),
            ],
        ),
        compiler_params=pltpu.CompilerParams(vmem_limit_bytes=56 * 1024 * 1024),
        cost_estimate=pl.CostEstimate(
            flops=20 * 10**9, bytes_accessed=30 * 10**6, transcendentals=10**6
        ),
        name="mix_forward",
    )(seq_lengths, tokens, weight_t, bias, conv)


def mix_backward(seq_lengths, grad_t, saved, conv, slots, marks):
    qkv_t, first, last, mark, value, inner, denom, middle, steps, inverse = saved
    width, tok_count = grad_t.shape
    heads = width // HEAD_DIM
    packed = slots * marks
    taps = conv.shape[1]
    args = (grad_t, qkv_t, first, last, mark, value, inner, denom, middle, steps, inverse, conv)
    whole = lambda shape: pl.BlockSpec(
        shape, lambda i, lens: (0,) * len(shape), pipeline_mode=pl.Buffered(1)
    )
    shapes = [((3 * width, tok_count), low), ((8, width), f32), ((heads, SUB), f32)]
    square = pltpu.VMEM((packed, width), f32)
    return pl.pallas_call(
        partial(mix_backward_kernel, slots, marks, taps),
        out_shape=[jax.ShapeDtypeStruct(s, t) for s, t in shapes],
        grid_spec=pltpu.PrefetchScalarGridSpec(
            num_scalar_prefetch=1,
            grid=(1,),
            in_specs=[whole(x.shape) for x in args],
            out_specs=[whole(s) for s, _ in shapes],
            scratch_shapes=[
                pltpu.VMEM((width, tok_count + 2 * SUB), low),
                pltpu.VMEM((width, tok_count + 2 * SUB), low),
                pltpu.VMEM((width, tok_count), low),
                pltpu.VMEM((width, tok_count), low),
                pltpu.VMEM((heads, SUB, 3 * SUB), f32),
                square, square, square, square,
                pltpu.VMEM((heads, taps), f32),
            ],
        ),
        compiler_params=pltpu.CompilerParams(vmem_limit_bytes=56 * 1024 * 1024),
        cost_estimate=pl.CostEstimate(
            flops=20 * 10**9, bytes_accessed=30 * 10**6, transcendentals=10**6
        ),
        name="mix_backward",
    )(seq_lengths, *args)


contract_rows = (((0,), (0,)), ((), ()))
contract_cols = (((1,), (1,)), ((), ()))
norm_eps = 1e-05


def split_up(x, dim, peers):
    before, after = (x.shape[:dim], x.shape[dim + 1 :])
    return jnp.moveaxis(x.reshape(*before, peers, -1, *after), dim, 0)


def sum_at_owner(x, axis, dim):
    peers = lax.axis_size(axis)
    tiles = lax.all_to_all(split_up(x, dim, peers), axis, 0, 0, tiled=True)
    return jnp.sum(tiles.astype(f32), axis=0)


def layer_norm(row_data, gain_vec, shift_vec):
    centre = row_data - jnp.mean(row_data, axis=1, keepdims=True)
    spread_row = jnp.mean(centre * centre, axis=1, keepdims=True)
    return centre * lax.rsqrt(spread_row + norm_eps) * gain_vec[None, :] + shift_vec[None, :]


def gelu_exact(values):
    return jax.nn.gelu(values, approximate=False)


def body(
    tokens,
    qkv_weight,
    qv_bias,
    conv_weight,
    out_weight,
    out_bias,
    norm1_gain,
    norm1_bias,
    ffn_in_weight,
    ffn_in_bias,
    ffn_out_weight,
    ffn_out_bias,
    norm2_gain,
    norm2_bias,
    cotangent,
    seq_lengths,
    segment_ids,
    landmark_bounds,
):
    tok_count, model_width = tokens.shape
    head_width = qkv_weight.shape[2]
    heads_here = head_width // HEAD_DIM
    head_total = conv_weight.shape[0]
    kernel_taps = conv_weight.shape[1]
    slots, marks = landmark_bounds.shape
    quarter = tok_count // lax.axis_size("heads")
    head_index = lax.axis_index("heads")
    own_start = head_index * quarter
    both = ("batch", "heads")
    own_rows_low = lax.dynamic_slice_in_dim(tokens, own_start, quarter, 0)
    own_tokens = own_rows_low.astype(f32)
    flat_qkv = qkv_weight.reshape(model_width, 3 * head_width)
    forward = mix_forward(
        seq_lengths, tokens, jnp.transpose(flat_qkv), qv_bias, conv_weight, slots, marks
    )
    qkv_t, first, last, mixed_t, mark, value, inner, denom, middle, steps, inverse, bound = forward
    bound_total = bound[0, 0]
    attn_part = lax.psum_scatter(
        lax.dot_general(mixed_t, out_weight, contract_rows, preferred_element_type=f32).astype(low),
        "heads",
        scatter_dimension=0,
        tiled=True,
    ).astype(f32)
    live_count = jnp.sum((seq_lengths > 0).astype(f32)) * heads_here
    first_res = own_tokens + attn_part + out_bias[None, :]
    norm1_out, norm1_pull = jax.vjp(layer_norm, first_res, norm1_gain, norm1_bias)
    norm1_low = norm1_out.astype(low)
    ff_own = ffn_out_weight.shape[0]
    bias_row = jnp.zeros((16, model_width), low).at[0, :ff_own].set(ffn_in_bias)
    whole_in = lax.all_gather(ffn_in_weight, both, axis=1, tiled=True)
    out_pack = lax.all_gather(jnp.concatenate([ffn_out_weight, bias_row], axis=0), both, axis=0)
    whole_out = out_pack[:, :ff_own].reshape(-1, model_width)
    whole_in_bias = out_pack[:, ff_own, :ff_own].reshape(-1)
    pre_act = (
        jnp.dot(norm1_low, whole_in, preferred_element_type=f32)
        + whole_in_bias.astype(f32)[None, :]
    )
    hidden_act, gelu_pull = jax.vjp(gelu_exact, pre_act)
    hidden_low = hidden_act.astype(low)
    ffn_result = jnp.dot(hidden_low, whole_out, preferred_element_type=f32) + ffn_out_bias[None, :]
    final_out, norm2_pull = jax.vjp(layer_norm, norm1_out + ffn_result, norm2_gain, norm2_bias)
    grad_second, grad_gain_two, grad_shift_two = norm2_pull(cotangent.astype(f32))
    grad_ffn_low = grad_second.astype(low)
    grad_ffn_bias = jnp.sum(grad_ffn_low.astype(f32), axis=0)
    down_term = lax.dot_general(
        hidden_low, grad_ffn_low, contract_rows, preferred_element_type=f32
    ).astype(low)
    grad_hidden = lax.dot_general(
        grad_ffn_low, whole_out, contract_cols, preferred_element_type=f32
    )
    grad_pre = gelu_pull(grad_hidden)[0].astype(low)
    grad_in_bias = jnp.sum(grad_pre.astype(f32), axis=0)
    up_term = lax.dot_general(
        norm1_low, grad_pre, contract_rows, preferred_element_type=f32
    ).astype(low)
    grad_norm1 = grad_second + lax.dot_general(
        grad_pre, whole_in, contract_cols, preferred_element_type=f32
    )
    grad_first, grad_gain_one, grad_shift_one = norm1_pull(grad_norm1)
    grad_attn_low = grad_first.astype(low)
    grad_out_bias = jnp.sum(grad_attn_low.astype(f32), axis=0)
    piece_rows = lax.all_gather(grad_attn_low, "heads", axis=0, tiled=True)
    grad_mix_t = lax.dot_general(
        out_weight, piece_rows, contract_cols, preferred_element_type=f32
    ).astype(low)
    grad_mix_t, down_term, up_term = lax.optimization_barrier((grad_mix_t, down_term, up_term))
    up_share = lax.psum_scatter(up_term, both, scatter_dimension=1, tiled=True).astype(f32)
    down_share = lax.psum_scatter(down_term, both, scatter_dimension=0, tiled=True).astype(f32)
    saved = (qkv_t, first, last, mark, value, inner, denom, middle, steps, inverse)
    grad_t, grad_bias, grad_conv = mix_backward(
        seq_lengths, grad_mix_t, saved, conv_weight, slots, marks
    )
    out_part = lax.dot_general(
        mixed_t, piece_rows, (((1,), (0,)), ((), ())), preferred_element_type=f32
    )
    grad_qv_own = grad_bias[:2]
    qkv_part = lax.dot_general(
        tokens, grad_t, (((0,), (1,)), ((), ())), preferred_element_type=f32
    ).reshape(model_width, 3, head_width)
    input_part = lax.psum_scatter(
        lax.dot_general(
            grad_t, flat_qkv, (((0,), (1,)), ((), ())), preferred_element_type=f32
        ).astype(low),
        "heads",
        scatter_dimension=0,
        tiled=True,
    ).astype(f32)
    input_grad = grad_first + input_part
    conv_full = lax.dynamic_update_slice_in_dim(
        jnp.zeros((head_total, kernel_taps), f32),
        grad_conv[:, :kernel_taps],
        head_index * heads_here,
        0,
    )
    bias_full = lax.dynamic_update_slice_in_dim(
        jnp.zeros((2, head_total * HEAD_DIM), f32), grad_qv_own, head_index * head_width, 1
    )
    qkv_share, out_share = (
        sum_at_owner(qkv_part.astype(low), "batch", 0),
        sum_at_owner(out_part.astype(low), "batch", 1),
    )
    vector_all = jnp.stack(
        [grad_ffn_bias, grad_gain_two, grad_shift_two, grad_gain_one, grad_shift_one, grad_out_bias]
    )
    in_bias_share, vector_share = (
        lax.psum_scatter(grad_in_bias, both, scatter_dimension=0, tiled=True),
        lax.psum_scatter(vector_all, both, scatter_dimension=1, tiled=True),
    )
    conv_sum, bias_sum, bound_all, count_all = lax.psum(
        (conv_full, bias_full, bound_total, live_count), both
    )
    conv_out = lax.dynamic_slice_in_dim(conv_sum, head_index * heads_here, heads_here, 0)
    bias_out = lax.dynamic_slice_in_dim(bias_sum, head_index * head_width, head_width, 1)
    condition = bound_all / count_all
    return (
        final_out.astype(low),
        input_grad,
        qkv_share,
        bias_out,
        conv_out,
        out_share,
        up_share,
        in_bias_share,
        down_share,
        vector_share,
        condition,
    )


def place():
    b, z = lax.axis_index("batch"), lax.axis_index("heads")
    core, x, y = b % 2, (b // 2) % 2, b // 4
    return b, z, b + 1 - 2 * core, b + 2 - 4 * x, b + 4 - 8 * y


def remote(src, dst, send, recv, device):
    return pltpu.make_async_remote_copy(
        src_ref=src,
        dst_ref=dst,
        send_sem=send,
        recv_sem=recv,
        device_id=device,
        device_id_type=pl.DeviceIdType.MESH,
    )


def greet(devices):
    barrier = pltpu.get_barrier_semaphore()
    for device in devices:
        pl.semaphore_signal(
            barrier, inc=1, device_id=device, device_id_type=pl.DeviceIdType.MESH
        )
    pl.semaphore_wait(barrier, len(devices))


def tail_kernel(
    len_ref,
    gt_hbm, wq_hbm, we_hbm, hid_hbm, pre_hbm, n1_hbm, gf_hbm, ga_hbm, mx_hbm, tok_hbm, first_hbm,
    sums_ref, bin_ref, qv_ref, conv_ref, bound_ref,
    input_ref, down_own, up_own, outw_own, qkvw_own, in_bias, vector_own, qv_own, conv_own, ratio,
    small_out,
    gt, wq, we, hid, pre, n1, gf, ga, mx, tok,
    q_in, r_out, r_in, s_in, out_down, out_up, full_outw, full_qkvw, acc_qkvw,
    core_down, core_up, core_outw, core_qkvw,
    one_down, one_up, one_outw, one_qkvw, two_down, two_up, two_outw, two_qkvw,
    e_down, e_up, e_outw, g_down, g_up, g_outw, h_down, h_up, h_outw, small_in,
    load_sem, q_send, q_recv, r_send, r_recv, t_send, t_recv, c_send, c_recv, x_send, x_recv, e_send, e_recv,
    g_send, g_recv, h_send, h_recv, s_send, s_recv,
):
    b, z, bc, bx, by = place()
    both = bx + by - b
    flip = bc - b
    peers = [(b, lax.rem(z + i, 4)) for i in (1, 2, 3)]
    issued = []
    loads = [
        pltpu.make_async_copy(src, dst, load_sem.at[n])
        for n, (src, dst) in enumerate(
            (
                (pre_hbm, pre), (n1_hbm, n1), (hid_hbm, hid), (gf_hbm, gf), (gt_hbm, gt),
                (wq_hbm, wq), (we_hbm, we), (mx_hbm, mx), (ga_hbm, ga), (tok_hbm, tok),
                (first_hbm, input_ref),
            )
        )
    ]
    for copy in loads:
        copy.start()
    greet(peers + [(bc, z), (bx, z), (by, z)])
    chunks, size = r_in.shape[1:3]
    quarter = chunks * size
    ff = down_own.shape[0]
    group = 4 * ff

    zf = z + 1 - 2 * (z % 2)
    zg = z + 2 - 4 * (z // 2)
    partners = ((bc, z), (bx, z), (by, z), (b, zf), (b, zg))

    def small_start(k):
        copy = remote(
            small_out.at[k], small_in.at[k], s_send.at[k], s_recv.at[k], partners[k]
        )
        copy.start()
        issued.append(copy)

    def small_event(k):
        ref = small_in.at[k]
        remote(ref, ref, s_send.at[k], s_recv.at[k], partners[k]).wait_recv()
        small_out[k + 1] = small_out[k] + small_in[k]
        if k < 4:
            small_start(k + 1)

    model = input_ref.shape[1]
    bias_rows = bin_ref.shape[1] // model
    at_vec, at_qv = bias_rows, bias_rows + 6
    heads, taps = conv_own.shape
    at_conv = at_qv + 8
    at_end = at_conv + 4 * heads
    width = qv_own.shape[1]
    small_out[0] = jnp.zeros(small_out.shape[1:], f32)
    for n in range(bias_rows):
        small_out[0, n : n + 1, :] = bin_ref[0:1, n * model : (n + 1) * model]
    small_out[0, at_vec : at_vec + 6, :] = sums_ref[0:6, :]
    live = jnp.int32(0)
    for n in range(len_ref.shape[0]):
        live = live + jnp.where(len_ref[n] > 0, heads, 0)
    lane = lax.broadcasted_iota(jnp.int32, (1, 128), 1)
    small_out[0, at_end : at_end + 1, 0:128] = jnp.where(
        lane == 0, bound_ref[0:1, :], jnp.where(lane == 1, live.astype(f32), 0.0)
    )
    for n in range(4):

        @pl.when(z == n)
        def _():
            for r in range(2):
                row = at_qv + 2 * n + r
                small_out[0, row : row + 1, :width] = qv_ref[r : r + 1, :]
            for r in range(heads):
                row = at_conv + heads * n + r
                small_out[0, row : row + 1, 0:128] = conv_ref[r : r + 1, :]

    small_start(0)

    is_end = (z == 0) | (z == 3)
    low_side = z < 2
    to_inner = jnp.where(low_side, 1, 2)
    across = jnp.where(z == 1, 2, 1)
    to_end = jnp.where(low_side, 0, 3)

    def owner(k):
        return jnp.where(low_side, 3 - k, k)

    def columns(who, c):
        return pl.ds(pl.multiple_of(who * quarter + c * size, size), size)

    def times(x, w):
        return lax.dot_general(x, w, (((0,), (0,)), ((), ())), preferred_element_type=f32)

    def part(who, c):
        return times(gt[:, columns(who, c)], wq[...])

    def q_copy(k, c):
        return remote(
            gt_hbm.at[:, columns(owner(k), c)], q_in.at[k, c], q_send.at[k, c], q_recv.at[k, c],
            (b, to_inner),
        )

    def q_wait(k, c):
        ref = q_in.at[k, c]
        remote(ref, ref, q_send.at[k, c], q_recv.at[k, c], (b, to_end)).wait_recv()

    def r_copy(k, c):
        return remote(
            r_out.at[k, c], r_in.at[k, c], r_send.at[k, c], r_recv.at[k, c], (b, across)
        )

    def t_copy(c):
        return remote(r_in.at[0, c], s_in.at[c], t_send.at[c], t_recv.at[c], (b, to_end))

    def first_hop(k, c):
        @pl.when(jnp.logical_not(is_end))
        def _():
            own = part(owner(k), c)
            q_wait(k, c)
            r_out[k, c] = (own + times(q_in[k, c], we[...])).astype(low)
            r_copy(k, c).start()

    def last_hop(c):
        @pl.when(jnp.logical_not(is_end))
        def _():
            own = part(to_end, c)
            r_copy(0, c).wait_recv()
            r_in[0, c] = (r_in[0, c].astype(f32) + own).astype(low)
            t_copy(c).start()

    cores = (core_down, core_up, core_outw, core_qkvw)
    ones = (one_down, one_up, one_outw, one_qkvw)
    twos = (two_down, two_up, two_outw, two_qkvw)
    outs = (out_down, out_up)
    left = (hid, pre)
    right = (gf, n1)

    def who(slot):
        return b + (slot % 2) * (bx - b) + (slot // 2) * (by - b)

    def term(n, owner):
        at = pl.ds(pl.multiple_of(owner * group, group), group)
        return lax.dot_general(
            left[n][:, at], right[n][...], (((0,), (0,)), ((), ())), preferred_element_type=f32
        )

    def core_copy(n, slot):
        if n < 2:
            src = outs[n].at[slot]
        elif n == 2:
            src = full_outw.at[:, who(slot) + flip]
        else:
            src = full_qkvw.at[who(slot) + flip]
        return remote(src, cores[n].at[slot], c_send.at[n, slot], c_recv.at[n, slot], (bc, z))

    def give(n, slot):
        if n < 2:
            value = term(n, who(slot) + flip).astype(low)
            outs[n][slot] = value.reshape(outs[n].shape[1:])
        core_copy(n, slot).start()

    def keep(n, slot):
        if n < 2:
            own = term(n, who(slot)).reshape(outs[n].shape[1:])
        elif n == 2:
            own = full_outw[:, who(slot)].astype(f32)
        else:
            own = full_qkvw[who(slot)].astype(f32)
        core_copy(n, slot).wait_recv()
        cores[n][slot] = (cores[n][slot].astype(f32) + own).astype(low)

    def side_copy(n, dst, src):
        partner = by if n % 2 == 0 else bx
        return remote(
            cores[n].at[src], ones[n].at[dst], x_send.at[n, dst], x_recv.at[n, dst], (partner, z)
        )

    def small_group(n):
        def one(i, _):
            give(n, 3 - i)
            return 0

        lax.fori_loop(0, 4, one, 0)

    def small_keep(n):
        def one(i, _):
            keep(n, 3 - i)
            return 0

        lax.fori_loop(0, 4, one, 0)
        side_copy(n, 1, 3).start()
        side_copy(n, 0, 2 if n % 2 == 0 else 1).start()

    def half(h, _):
        def one(i, _):
            slot_up, slot_down = 3 - 2 * i - h, 3 - i - 2 * h
            give(1, slot_up)
            give(0, slot_down)
            keep(1, slot_up)

            @pl.when(h == 0)
            def _():
                side_copy(1, 1 - i, slot_up).start()

            keep(0, slot_down)

            @pl.when(h == 0)
            def _():
                side_copy(0, 1 - i, slot_down).start()

            return 0

        lax.fori_loop(0, 2, one, 0)

        @pl.when(h == 0)
        def _():
            for n in (4, 5, 6):
                loads[n].wait()
            first_hop(0, 0)

        return 0

    def one_event(n):
        second = 1 if n % 2 == 0 else 2
        partner, other = (by, bx) if n % 2 == 0 else (bx, by)
        ref = ones[n].at[1]
        remote(ref, ref, x_send.at[n, 1], x_recv.at[n, 1], (partner, z)).wait_recv()
        ones[n][1] = (ones[n][1].astype(f32) + cores[n][second].astype(f32)).astype(low)
        copy = remote(ones[n].at[1], twos[n], x_send.at[n, 2], x_recv.at[n, 2], (other, z))
        copy.start()
        issued.append(copy)

    e_bufs = (e_down, e_up, e_outw)
    g_bufs = (g_down, g_up, g_outw)
    h_bufs = (h_down, h_up, h_outw)

    def e_copy(n, k):
        return remote(
            twos[n].at[owner(k)], e_bufs[n].at[k], e_send.at[n, k], e_recv.at[n, k], (b, to_inner)
        )

    def e_wait(n, k):
        ref = e_bufs[n].at[k]
        remote(ref, ref, e_send.at[n, k], e_recv.at[n, k], (b, to_end)).wait_recv()

    def g_copy(n, k):
        return remote(
            e_bufs[n].at[k], g_bufs[n].at[k], g_send.at[n, k], g_recv.at[n, k], (b, across)
        )

    def h_copy(n):
        return remote(g_bufs[n].at[0], h_bufs[n], h_send.at[n], h_recv.at[n], (b, to_end))

    def two_event(n):
        partner, other = (by, bx) if n % 2 == 0 else (bx, by)
        ref = ones[n].at[0]
        remote(ref, ref, x_send.at[n, 0], x_recv.at[n, 0], (partner, z)).wait_recv()
        ref = twos[n]
        remote(ref, ref, x_send.at[n, 2], x_recv.at[n, 2], (other, z)).wait_recv()
        own = ones[n][0].astype(f32) + cores[n][0].astype(f32)
        if n == 3:
            qkvw_own[...] = twos[n][...].astype(f32) + own
            return
        twos[n][...] = (twos[n][...].astype(f32) + own).astype(low)

    def line_start(n, k):
        @pl.when(is_end)
        def _():
            e_copy(n, k).start()

    def line_across(n, k):
        @pl.when(jnp.logical_not(is_end))
        def _():
            e_wait(n, k)
            e_bufs[n][k] = (
                e_bufs[n][k].astype(f32) + twos[n][owner(k)].astype(f32)
            ).astype(low)
            g_copy(n, k).start()

    def line_back(n):
        @pl.when(jnp.logical_not(is_end))
        def _():
            g_copy(n, 0).wait_recv()
            g_bufs[n][0] = (
                g_bufs[n][0].astype(f32) + twos[n][to_end].astype(f32)
            ).astype(low)
            h_copy(n).start()

    def end_event(n):
        def write(value):
            out = (down_own, up_own, outw_own)[n]
            out[...] = jnp.transpose(value) if n > 0 else value

        @pl.when(is_end)
        def _():
            ref = h_bufs[n]
            remote(ref, ref, h_send.at[n], h_recv.at[n], (b, to_inner)).wait_recv()
            write(twos[n][z].astype(f32) + h_bufs[n][...].astype(f32))
            for k in range(3):
                e_copy(n, k).wait_send()

        @pl.when(jnp.logical_not(is_end))
        def _():
            g_copy(n, 1).wait_recv()
            e_wait(n, 2)
            write(
                twos[n][z].astype(f32)
                + g_bufs[n][1].astype(f32)
                + e_bufs[n][2].astype(f32)
            )
            for k in range(2):
                g_copy(n, k).wait_send()
            h_copy(n).wait_send()

    def projections():
        on, oh = full_outw.shape[2:]
        for s in range(4):
            value = jnp.transpose(mul(mx[s], ga[...]))
            full_outw[s] = value.astype(low).reshape(full_outw.shape[1:])
        acc_qkvw[...] = jnp.zeros_like(acc_qkvw)
        span = quarter

        def one(n, _):
            at = pl.ds(pl.multiple_of(n * span, span), span)
            acc_qkvw[...] += mul(gt[:, at], tok[at, :])
            return 0

        lax.fori_loop(0, 4, one, 0)
        full_qkvw[...] = jnp.transpose(acc_qkvw[...]).astype(low).reshape(full_qkvw.shape)

    @pl.when(is_end)
    def _():
        for k in range(3):
            for c in range(chunks):
                q_copy(k, c).start()

    for n in range(4):
        loads[n].wait()

    lax.fori_loop(0, 2, half, 0)
    first_hop(0, 1)
    one_event(1)
    one_event(0)
    first_hop(0, 2)
    last_hop(0)
    for n in (7, 8, 9):
        loads[n].wait()
    projections()
    first_hop(1, 0)
    last_hop(1)
    small_group(2)
    small_group(3)
    small_event(0)
    first_hop(1, 1)
    last_hop(2)
    small_keep(2)
    small_keep(3)
    small_event(1)
    first_hop(1, 2)
    two_event(1)
    line_start(1, 0)
    two_event(0)
    line_start(0, 0)
    line_start(1, 1)
    line_start(0, 1)
    small_event(2)
    one_event(2)
    one_event(3)
    small_event(3)
    two_event(2)
    for k in range(3):
        line_start(2, k)
    line_start(1, 2)
    line_start(0, 2)
    two_event(3)
    small_event(4)
    loads[10].wait()

    def own_rows(c, _):
        rows = pl.ds(pl.multiple_of(c * size, size), size)
        input_ref[rows, :] += part(z, c)

        @pl.when(is_end)
        def _():
            ref = s_in.at[c]
            remote(ref, ref, t_send.at[c], t_recv.at[c], (b, to_inner)).wait_recv()
            input_ref[rows, :] += s_in[c].astype(f32)

        @pl.when(jnp.logical_not(is_end))
        def _():
            r_copy(1, c).wait_recv()
            q_wait(2, c)
            input_ref[rows, :] += r_in[1, c].astype(f32) + times(q_in[2, c], we[...])

        return 0

    lax.fori_loop(0, chunks, own_rows, 0)
    for n, k in ((1, 0), (0, 0), (1, 1), (0, 1), (2, 0), (2, 1)):
        line_across(n, k)
        if k == 1:
            line_back(n)
    for n in (1, 0, 2):
        end_event(n)

    @pl.when(is_end)
    def _():
        for k in range(3):
            for c in range(chunks):
                q_copy(k, c).wait_send()

    @pl.when(jnp.logical_not(is_end))
    def _():
        for c in range(chunks):
            r_copy(0, c).wait_send()
            r_copy(1, c).wait_send()
            t_copy(c).wait_send()

    final = small_out.at[5]
    in_bias[...] = jnp.zeros_like(in_bias)
    index = b * 4 + z
    per_row = model // ff
    for n in range(bias_rows):

        @pl.when(index // per_row == n)
        def _():
            row = pltpu.roll(final[n : n + 1, :], (model - (index % per_row) * ff) % model, 1)
            in_bias[...] = row[:, :ff]

    share = vector_own.shape[1]
    vectors = final[at_vec : at_vec + 6, :]
    vector_own[...] = pltpu.roll(vectors, (model - index * share) % model, 1)[:, :share]
    for n in range(4):

        @pl.when(z == n)
        def _():
            qv_own[...] = final[at_qv + 2 * n : at_qv + 2 * n + 2, :width]
            conv_own[...] = final[at_conv + heads * n : at_conv + heads * (n + 1), :taps]

    ratio[...] = final[at_end : at_end + 1, 0:1] / final[at_end : at_end + 1, 1:2]

    for n in range(4):
        for dst in range(2):
            side_copy(n, dst, dst).wait_send()
        for slot in range(4):
            core_copy(n, slot).wait_send()
    for copy in issued:
        copy.wait_send()


def tail(
    lengths, gt, wq, we, hid, pre, n1, gf, ga, mx, tok, first, sums, bins, qv_grad, conv_grad, bound,
    taps,
):
    quarter, model = first.shape
    chunks = 3
    size = quarter // chunks
    ff = hid.shape[1] // 32
    width = mx.shape[1]
    heads = width // HEAD_DIM
    on, oh = model // 8, width
    qn, qh = model // 8, gt.shape[0]
    blocks = ((4, ff, model), (4, ff, model), (4, on, oh), (qn, qh))
    own = lambda *s: jax.ShapeDtypeStruct(s, f32)
    vm = lambda *s: pltpu.VMEM(s, low)
    dma = pltpu.SemaphoreType.DMA
    sources = (gt, wq, we, hid, pre, n1, gf, ga, mx, tok)
    small = -(-(bins.shape[1] // model + 15 + 4 * heads) // 8) * 8
    vmem = pl.BlockSpec(memory_space=pltpu.VMEM)
    return pl.pallas_call(
        tail_kernel,
        out_shape=[
            own(quarter, model), own(ff, model), own(model, ff), own(oh, on), own(qn, qh),
            own(1, ff), own(6, model // 32), own(2, width), own(heads, taps), own(1, 1),
        ],
        in_specs=[pl.BlockSpec(memory_space=pltpu.SMEM)]
        + [pl.BlockSpec(memory_space=pl.ANY)] * 11
        + [vmem] * 5,
        out_specs=[vmem] * 10,
        scratch_shapes=[
            pltpu.VMEM((6, small, model), f32),
            *[vm(*x.shape) for x in sources],
            vm(3, chunks, qh, size), vm(2, chunks, size, model), vm(2, chunks, size, model),
            vm(chunks, size, model),
            vm(4, *blocks[0]), vm(4, *blocks[1]),
            vm(4, 8, on, oh), vm(8, qn, qh), pltpu.VMEM((qh, model), f32),
            *[vm(4, *s) for s in blocks],
            *[vm(2, *s) for s in blocks],
            *[vm(*s) for s in blocks],
            *[vm(3, *s[1:]) for s in blocks[:3]],
            *[vm(2, *s[1:]) for s in blocks[:3]],
            *[vm(*s[1:]) for s in blocks[:3]],
            pltpu.VMEM((5, small, model), f32),
            dma((11,)),
            dma((3, chunks)), dma((3, chunks)), dma((2, chunks)), dma((2, chunks)),
            dma((chunks,)), dma((chunks,)), dma((4, 4)), dma((4, 4)),
            dma((4, 3)), dma((4, 3)), dma((3, 3)), dma((3, 3)), dma((3, 2)), dma((3, 2)),
            dma((3,)), dma((3,)), dma((5,)), dma((5,)),
        ],
        compiler_params=pltpu.CompilerParams(
            collective_id=3, has_side_effects=True, vmem_limit_bytes=63 * 1024 * 1024
        ),
        name="tail",
    )(lengths, *sources, first, sums, bins, qv_grad, conv_grad, bound)


def cumulative(x):
    t = 1.0 / (1.0 + 0.23164189 * jnp.abs(x))
    density = jnp.exp(-0.5 * x * x) * 0.3989422804
    poly = t * (
        0.319381530 + t * (-0.356563782 + t * (1.781477937 + t * (-1.821255978 + t * 1.330274429)))
    )
    upper = density * poly
    return jnp.where(x >= 0.0, 1.0 - upper, upper), density


def normed(x):
    centre = x - jnp.mean(x, axis=1, keepdims=True)
    scale = lax.rsqrt(jnp.mean(centre * centre, axis=1, keepdims=True) + norm_eps)
    return centre * scale, scale


def norm_back(grad, gain, rows, scale):
    e = grad * gain
    return scale * (
        e - jnp.mean(e, axis=1, keepdims=True) - rows * jnp.mean(e * rows, axis=1, keepdims=True)
    )


def middle_kernel(
    share,
    mixed_ref, own0, own1, own2, own3, tok_hbm, cot_hbm,
    vec_ref,
    out_hbm, first_hbm, attn_hbm, hidden_hbm, pre_hbm, norm_hbm, ffn_hbm, all_ref, grad_ref,
    sums_ref, bin_ref,
    out_ref, first_ref, attn_ref, hidden_ref, pre_ref, norm_ref, ffn_ref, tok_ref, cot_ref,
    packs, wof, wo, slope, total, n1_ref, scale_ref, turned,
    a_send, a_recv, f_send, f_recv, s_send, s_recv, p_send, p_recv, g_send, g_recv,
    own_sem, own_turn, out_sem,
):
    b, z, bc, bx, by = place()
    both = bx + by - b
    flip = bc - b
    peers = [(b, lax.rem(z + i, 4)) for i in (1, 2, 3)]
    width, quarter = all_ref.shape[1:]
    model = tok_hbm.shape[1]
    owns = (own0, own1, own2, own3)
    origins = [lax.rem(z + 4 - i, 4) for i in range(4)]
    size = turned.shape[2]
    tiles = quarter // size
    issued = []

    def own_columns(n):
        return pl.ds(pl.multiple_of(n * quarter, quarter), quarter)

    local = [
        pltpu.make_async_copy(own, packs.at[b, origin], own_sem.at[i])
        for i, (own, origin) in enumerate(zip(owns, origins))
    ]
    local.append(
        pltpu.make_async_copy(mixed_ref.at[:, own_columns(z)], all_ref.at[z], own_sem.at[4])
    )
    local.append(
        pltpu.make_async_copy(
            tok_hbm.at[pl.ds(pl.multiple_of(z * quarter, quarter), quarter)], tok_ref, own_sem.at[5]
        )
    )
    cot_load = pltpu.make_async_copy(cot_hbm, cot_ref, own_sem.at[6])
    for copy in local:
        copy.start()
    cot_load.start()
    greet(peers + [(bc, z), (bx, z), (by, z)])

    ff = (packs.shape[2] - 32) // 2
    half = ff // 2
    pieces = ((2 * ff, 32), (0, half), (half, half), (ff, ff))
    through_y = (True, True, True, False)
    count = len(pieces)

    def rows_of(n):
        return pl.ds(*pieces[n])

    def mix_copy(r, i):
        to = lax.rem(z + i, 4)
        src = mixed_ref.at[:, pl.ds(pl.multiple_of(to * quarter + r * size, size), size)]
        return remote(
            src, all_ref.at[z, :, pl.ds(r * size, size)], a_send.at[r, i - 1], a_recv.at[r, i - 1],
            (b, to),
        )

    def side(n, axis):
        out = []
        for i in range(4):
            out.append(
                remote(
                    owns[i].at[rows_of(n)], packs.at[b, origins[i], rows_of(n)],
                    f_send.at[n, axis, i], f_recv.at[n, axis, i], (by if axis else bx, z),
                )
            )
        return out

    def side_start(n):
        for axis in (0, 1):
            for copy in side(n, axis):
                copy.start()
                issued.append(copy)

    def block(n, who):
        return packs.at[who, :, rows_of(n)]

    def corner(n):
        who, device = (bx, by) if through_y[n] else (by, bx)
        return remote(block(n, who), block(n, who), s_send.at[n], s_recv.at[n], (device, z))

    def mate(n, slot, who):
        return remote(
            block(n, who), block(n, who), p_send.at[n, slot], p_recv.at[n, slot], (bc, z)
        )

    def mate_start(n, slot, who):
        mate(n, slot, who).start()

    def side_wait(n, axis):
        who = by if axis else bx
        for i in range(4):
            ref = packs.at[who, origins[i], rows_of(n)]
            remote(
                ref, ref, f_send.at[n, axis, i], f_recv.at[n, axis, i], (who, z)
            ).wait_recv()
        if through_y[n] == (axis == 0):
            corner(n).start()
        mate_start(n, 1 + axis, who)

    def corner_wait(n):
        device = by if through_y[n] else bx
        ref = block(n, both)
        remote(ref, ref, s_send.at[n], s_recv.at[n], (device, z)).wait_recv()
        mate_start(n, 3, both)

    def mate_wait(n, slot, who):
        mate(n, slot, who + flip).wait_recv()

    side_start(0)
    side_start(1)
    for r in range(tiles):
        for i in (1, 2, 3):
            copy = mix_copy(r, i)
            copy.start()
            issued.append(copy)
    for copy in local:
        copy.wait()
    for n in range(count):
        mate_start(n, 0, b)
    out_bias, gain1, shift1, down_bias, gain2, shift2 = [
        vec_ref[n : n + 1, :] for n in range(6)
    ]
    sums_ref[...] = jnp.zeros_like(sums_ref)
    bin_ref[...] = jnp.zeros_like(bin_ref)
    total[...] = jnp.zeros_like(total)
    side_wait(0, 0)
    side_wait(0, 1)
    side_start(2)
    side_start(3)
    corner_wait(0)
    for slot, who in enumerate((b, bx, by, both)):
        mate_wait(0, slot, who)
    group = 4 * ff
    for q in range(8):
        for s in range(4):
            wof[pl.ds(s * width + q * share, share), :] = packs[
                q, s, pl.ds(2 * ff, share), :
            ].astype(f32)
    wo[...] = wof[...].astype(low).reshape(wo.shape)
    for q in range(8):
        row = jnp.zeros((1, group), f32)
        for s in range(4):
            row = row + packs[q, s, 2 * ff + share : 2 * ff + share + 1, :group].astype(f32)
        bin_ref[1:2, q * group : (q + 1) * group] = row

    def row_sum(n, x):
        sums_ref[n : n + 1, :] += jnp.sum(x, axis=0, keepdims=True)

    def first_rows(r, _):
        rows = pl.ds(pl.multiple_of(r * size, size), size)

        @pl.when(r == 1)
        def _():
            side_wait(1, 0)
            side_wait(1, 1)

        @pl.when(r == 2)
        def _():
            side_wait(2, 0)
            side_wait(2, 1)

        for i in (1, 2, 3):
            ref = all_ref.at[origins[i], :, rows]
            remote(
                ref, ref, a_send.at[r, i - 1], a_recv.at[r, i - 1], (b, origins[i])
            ).wait_recv()
        attn = jnp.zeros((size, model), f32)
        for s in range(4):
            attn = attn + lax.dot_general(
                all_ref[s, :, rows], wo[s], (((0,), (0,)), ((), ())), preferred_element_type=f32
            )
        n1, scale1 = normed(tok_ref[rows, :].astype(f32) + attn + out_bias)
        n1_ref[rows, :] = n1
        scale_ref[rows, :] = jnp.broadcast_to(scale1, (size, scale_ref.shape[1]))
        norm_ref[rows, :] = (n1 * gain1 + shift1).astype(low)
        return 0

    span = 2 * group

    def weights(c, start):
        return jnp.concatenate(
            [
                packs[2 * c + n, :, pl.ds(start, ff), :].reshape(group, model)
                for n in range(2)
            ],
            axis=0,
        )

    def tile_rows(r):
        return pl.ds(pl.multiple_of(r * size, size), size)

    def feed(who):
        c = who // 2
        lanes = pl.ds(pl.multiple_of(c * span, span), span)

        def one(r, _):
            rows = tile_rows(r)
            act = mul_t(norm_ref[rows, :], weights(c, 0)) + bin_ref[1:2, lanes]
            phi, density = cumulative(act)
            hidden = (act * phi).astype(low)
            hidden_ref[rows, lanes] = hidden
            slope[rows, lanes] = phi + act * density
            total[rows, :] += mul(hidden, weights(c, ff))
            return 0

        lax.fori_loop(0, tiles, one, 0)

    lax.fori_loop(0, tiles, first_rows, 0)

    def group_step(k, _):
        def mates(slot, who):
            for n in range(1, count):
                mate_wait(n, slot, who)

        @pl.when(k == 0)
        def _():
            mates(0, b)

        @pl.when(k == 1)
        def _():
            side_wait(3, 0)
            side_wait(3, 1)
            mates(1, bx)

        @pl.when(k == 2)
        def _():
            corner_wait(1)
            mates(2, by)

        @pl.when(k == 3)
        def _():
            corner_wait(2)
            corner_wait(3)
            mates(3, both)

        feed(b + (k % 2) * (bx - b) + (k // 2) * (by - b))
        return 0

    lax.fori_loop(0, 4, group_step, 0)

    def turn_copy(r, i):
        to = lax.rem(z + i, 4)
        src = turned.at[r, pl.ds(pl.multiple_of(to * width, width), width)]
        dst = grad_ref.at[:, pl.ds(pl.multiple_of(z * quarter + r * size, size), size)]
        return remote(src, dst, g_send.at[r, i - 1], g_recv.at[r, i - 1], (b, to))

    def turn_own(r):
        src = turned.at[r, pl.ds(pl.multiple_of(z * width, width), width)]
        dst = grad_ref.at[:, pl.ds(pl.multiple_of(z * quarter + r * size, size), size)]
        return pltpu.make_async_copy(src, dst, own_turn.at[r])

    stores = (
        (out_ref, out_hbm), (first_ref, first_hbm), (attn_ref, attn_hbm), (pre_ref, pre_hbm),
        (ffn_ref, ffn_hbm), (hidden_ref, hidden_hbm), (norm_ref, norm_hbm),
    )

    def store(r, n):
        src, dst = stores[n]
        rows = tile_rows(r)
        return pltpu.make_async_copy(src.at[rows], dst.at[rows], out_sem.at[r, n])

    cot_load.wait()

    def row_tile(r, _):
        rows = tile_rows(r)
        n1 = n1_ref[rows, :]
        norm1 = n1 * gain1 + shift1
        n2, scale2 = normed(norm1 + total[rows, :] + down_bias)
        out_ref[rows, :] = (n2 * gain2 + shift2).astype(low)
        cot = cot_ref[rows, :].astype(f32)
        row_sum(1, cot * n2)
        row_sum(2, cot)
        grad2 = norm_back(cot, gain2, n2, scale2)
        grad_low = grad2.astype(low)
        ffn_ref[rows, :] = grad_low
        row_sum(0, grad_low.astype(f32))
        total[rows, :] = grad2

        def backward(c, _):
            lanes = pl.ds(pl.multiple_of(c * span, span), span)
            grad = (slope[rows, lanes] * mul_t(grad_low, weights(c, ff))).astype(low)
            pre_ref[rows, lanes] = grad
            bin_ref[0:1, lanes] += jnp.sum(grad.astype(f32), axis=0, keepdims=True)
            total[rows, :] += mul(grad, weights(c, 0))
            return 0

        lax.fori_loop(0, 4, backward, 0)
        grad1 = total[rows, :]
        row_sum(3, grad1 * n1)
        row_sum(4, grad1)
        first = norm_back(grad1, gain1, n1, scale_ref[rows, 0:1])
        first_ref[rows, :] = first
        attn_low = first.astype(low)
        attn_ref[rows, :] = attn_low
        row_sum(5, attn_low.astype(f32))
        for s in range(4):
            turned[r, pl.ds(s * width, width), :] = mul_t(wo[s], attn_low).astype(low)
        for i in (1, 2, 3):
            turn_copy(r, i).start()
        turn_own(r).start()
        for n in range(len(stores)):
            store(r, n).start()
        return 0

    lax.fori_loop(0, tiles, row_tile, 0)

    def finish(r, _):
        for i in (1, 2, 3):
            source = origins[i]
            ref = grad_ref.at[:, pl.ds(pl.multiple_of(source * quarter + r * size, size), size)]
            remote(ref, ref, g_send.at[r, i - 1], g_recv.at[r, i - 1], (b, source)).wait_recv()
            turn_copy(r, i).wait_send()
        turn_own(r).wait()
        for n in range(len(stores)):
            store(r, n).wait()
        return 0

    lax.fori_loop(0, tiles, finish, 0)
    for n in range(count):
        corner(n).wait_send()
        for slot, who in enumerate((b, bx, by, both)):
            mate(n, slot, who).wait_send()
    for copy in issued:
        copy.wait_send()


def ffn_middle(mixed_t, packs, tokens, cot, vectors, ff, share):
    width, tok_count = mixed_t.shape
    quarter, model = tok_count // 4, tokens.shape[1]
    size = quarter // 3
    rows = packs[0].shape[0]
    shape = jax.ShapeDtypeStruct
    vmem = pl.BlockSpec(memory_space=pltpu.VMEM)
    hbm = pl.BlockSpec(memory_space=pl.ANY)
    dma = pltpu.SemaphoreType.DMA
    kept = [
        ((quarter, model), low),
        ((quarter, model), f32),
        ((quarter, model), low),
        ((quarter, 32 * ff), low),
        ((quarter, 32 * ff), low),
        ((quarter, model), low),
        ((quarter, model), low),
    ]
    return pl.pallas_call(
        partial(middle_kernel, share),
        out_shape=[shape(*x) for x in kept]
        + [
            shape((4, width, quarter), low),
            shape((width, tok_count), low),
            shape((8, model), f32),
            shape((8, 32 * ff), f32),
        ],
        in_specs=[hbm] + [vmem] * 4 + [hbm] * 2 + [vmem],
        out_specs=[hbm] * 7 + [vmem, hbm, vmem, vmem],
        scratch_shapes=[pltpu.VMEM(*x) for x in kept]
        + [
            pltpu.VMEM((quarter, model), low),
            pltpu.VMEM((quarter, model), low),
            pltpu.VMEM((8, 4, rows, model), low),
            pltpu.VMEM((4 * width, model), f32),
            pltpu.VMEM((4, width, model), low),
            pltpu.VMEM((quarter, 32 * ff), f32),
            pltpu.VMEM((quarter, model), f32),
            pltpu.VMEM((quarter, model), f32),
            pltpu.VMEM((quarter, 128), f32),
            pltpu.VMEM((3, 4 * width, size), low),
            dma((3, 3)), dma((3, 3)), dma((4, 2, 4)), dma((4, 2, 4)), dma((4,)), dma((4,)),
            dma((4, 4)), dma((4, 4)), dma((3, 3)), dma((3, 3)),
            dma((7,)), dma((3,)), dma((3, 7)),
        ],
        compiler_params=pltpu.CompilerParams(
            collective_id=1, has_side_effects=True, vmem_limit_bytes=63 * 1024 * 1024
        ),
        name="middle",
    )(mixed_t, *packs, tokens, cot, vectors)


def settle_kernel(*refs):
    count = len(refs) // 2
    for n in range(count):
        refs[count + n][...] = refs[n][...]


def settle(*arrays):
    vmem = pl.BlockSpec(memory_space=pltpu.VMEM)
    return pl.pallas_call(
        settle_kernel,
        out_shape=[jax.ShapeDtypeStruct(x.shape, x.dtype) for x in arrays],
        in_specs=[vmem] * len(arrays),
        out_specs=[vmem] * len(arrays),
        name="settle",
    )(*arrays)


def slice_body(
    tokens,
    qkv_weight,
    qv_bias,
    conv_weight,
    out_weight,
    out_bias,
    norm1_gain,
    norm1_bias,
    ffn_in_weight,
    ffn_in_bias,
    ffn_out_weight,
    ffn_out_bias,
    norm2_gain,
    norm2_bias,
    cotangent,
    seq_lengths,
    segment_ids,
    landmark_bounds,
):
    model = tokens.shape[1]
    width = qkv_weight.shape[2]
    kernel_taps = conv_weight.shape[1]
    slots, marks = landmark_bounds.shape
    z = lax.axis_index("heads")
    b = lax.axis_index("batch")
    weight_t = jnp.transpose(qkv_weight.reshape(model, 3 * width))
    ff_own = ffn_out_weight.shape[0]
    share = width // 8
    bias_row = lax.dynamic_update_slice_in_dim(
        jnp.zeros((4 * ff_own,), low), ffn_in_bias, z * ff_own, 0
    )
    misc_own = jnp.concatenate(
        [
            lax.dynamic_slice_in_dim(out_weight, b * share, share, 0),
            jnp.zeros((32 - share, model), low).at[0, : 4 * ff_own].set(bias_row),
        ],
        axis=0,
    )
    pack = jnp.concatenate([jnp.transpose(ffn_in_weight), ffn_out_weight, misc_own], axis=0)
    packs = [pack] + [
        lax.ppermute(pack, "heads", [(n, (n + i) % 4) for n in range(4)]) for i in (1, 2, 3)
    ]
    forward = mix_forward(
        seq_lengths, tokens, weight_t, qv_bias, conv_weight, slots, marks
    )
    qkv_t, first, last, mixed_t, mark, value, inner, denom, middle, steps, inverse, bound = forward
    vectors = jnp.stack(
        [out_bias, norm1_gain, norm1_bias, ffn_out_bias, norm2_gain, norm2_bias]
    )
    (
        final_low, grad_first, grad_attn_low, hidden_low, grad_pre, norm1_low, grad_ffn_low,
        mixed_all, grad_mix_t, vector_sums, bias_sums,
    ) = ffn_middle(mixed_t, packs, tokens, cotangent, vectors, ff_own, share)
    saved = (qkv_t, first, last, mark, value, inner, denom, middle, steps, inverse)
    held, grad_mix_t = lax.optimization_barrier((weight_t, grad_mix_t))
    weight_end = lax.ppermute(held, "heads", [(0, 1), (3, 2)])
    grad_t, grad_bias, grad_conv = mix_backward(
        seq_lengths, grad_mix_t, saved, conv_weight, slots, marks
    )
    (
        input_grad, down_share, up_share, out_share, qkv_share,
        in_bias_share, vector_share, bias_out, conv_out, condition,
    ) = tail(
        seq_lengths, grad_t, weight_t, weight_end, hidden_low, grad_pre, norm1_low, grad_ffn_low,
        grad_attn_low, mixed_all, tokens, grad_first, vector_sums, bias_sums, grad_bias,
        grad_conv, bound, kernel_taps,
    )
    (
        final_low, input_grad, down_share, up_share, out_share, qkv_share,
        in_bias_share, vector_share, bias_out, conv_out, condition,
    ) = settle(
        final_low, input_grad, down_share, up_share, out_share, qkv_share,
        in_bias_share, vector_share, bias_out, conv_out, condition,
    )
    return (
        final_low,
        input_grad,
        qkv_share.reshape(model // 8, 3, width),
        bias_out,
        conv_out,
        out_share,
        up_share,
        in_bias_share.reshape(ff_own),
        down_share,
        vector_share,
        condition.reshape(()),
    )


def solution(mesh):
    chosen = slice_body if dict(mesh.shape) == {"batch": 8, "heads": 4} else body
    in_specs = (
        P("batch", None),
        P(None, None, "heads"),
        P(),
        P(),
        P("heads", None),
        P(),
        P(),
        P(),
        P(None, ("batch", "heads")),
        P(("batch", "heads")),
        P(("batch", "heads"), None),
        P(),
        P(),
        P(),
        P(("batch", "heads"), None),
        P("batch"),
        P("batch"),
        P("batch", None),
    )
    out_specs = (
        P(("batch", "heads"), None),
        P(("batch", "heads"), None),
        P("batch", None, "heads"),
        P(None, "heads"),
        P("heads", None),
        P("heads", "batch"),
        P(None, ("batch", "heads")),
        P(("batch", "heads")),
        P(("batch", "heads"), None),
        P(None, ("batch", "heads")),
        P(),
    )
    return jax.shard_map(chosen, mesh=mesh, in_specs=in_specs, out_specs=out_specs, check_vma=False)
```

profile of v0, /device:TPU:0, one launch (start us, length us, event | category | flops | bytes accessed | tf_op | source)
XLA Modules:
  0.0 288.0 jit_solution(8721747442708807370)
XLA Ops:
  0.6 0.0 copy-start
  0.7 0.9 copy-done
  1.6 0.8 dynamic_update_slice.6
  2.4 1.0 fusion.1.own0
  3.4 0.0 copy-start.1
  3.4 5.2 %collective-permute-start.2 = (bf16[224,768]{1,0:T(8,128)(2,1)S(1)}, bf16[224,768]{1,0:T(8,128)(2,1)S(1)}, u32[]{:S(2)}, u32[]{:S(2)}) collective-permute-start(bf16[224,768]{1,0:T(8,128)(2,1)S(1)} %fusion.1.own0), channel_id=1, source_target_pairs={{0,3},{1,0},{2,1},{3,2},{4,7},{5,4},{6,5},{7,6},{8,11},{9,8},{10,9... | collective-permute-start | bytes 1032200 | tf_op jit(solution)/shard_map/ppermute | solution.py:1875
  8.6 0.0 collective-permute-start.1
  8.6 1.0 collective-permute-start
  9.6 0.0 copy-start.6
  9.6 0.0 copy-start.7
  9.6 0.0 copy-start.8
  9.6 0.0 copy-start.9
  9.6 0.0 copy-start.10
  9.7 0.0 copy-start.11
  9.7 32.1 %mix_forward.1 = (bf16[576,3072]{1,0:T(8,128)(2,1)}, bf16[192,3072]{1,0:T(8,128)(2,1)}, bf16[192,3072]{1,0:T(8,128)(2,1)}, bf16[192,3072]{1,0:T(8,128)(2,1)}, f3...) custom-call(s32[3]{0:T(128)} %len_ref.5, ...), custom_call_target="tpu_custom_call" | custom-call | flops 20000000000 | bytes 30000000 | tf_op jit(solution)/shard_map/mix_forward/pallas_call | solution.py:629
  41.8 0.0 copy-done.1
  41.8 0.0 copy-done.6
  41.8 0.0 copy-done.7
  41.8 0.0 copy-done.8
  41.8 0.0 copy-done.9
  41.8 0.0 copy-done.10
  41.9 0.0 copy-done.11
  41.9 0.6 stack.27.vec_ref
  42.5 0.0 collective-permute-done.2.own3
  42.5 0.0 copy-start.3
  42.5 0.0 collective-permute-done.1.own2
  42.5 0.0 copy-start.4
  42.6 0.0 collective-permute-done.own1
  42.6 0.0 copy-start.5
  42.6 0.8 copy-done.5
  43.3 0.0 copy-done.3
  43.4 0.1 copy-done.4
  43.5 91.0 %middle.1 = (bf16[768,768]{1,0:T(8,128)(2,1)}, f32[768,768]{1,0:T(8,128)}, bf16[768,768]{1,0:T(8,128)(2,1)}, bf16[768,3072]{1,0:T(8,128)(2,1)}, bf16[768,3072]{1...) custom-call(bf16[192,3072]{1,0:T(8,128)(2,1)} %get-tuple-element.72., ...), custom_call_target="tpu_custom_call" | custom-call | tf_op jit(solution)/shard_map/middle/pallas_call | solution.py:1783
  134.5 5.5 %collective-permute-start.3 = (bf16[576,768]{1,0:T(8,128)(2,1)}, bf16[576,768]{1,0:T(8,128)(2,1)}, u32[]{:S(2)}, u32[]{:S(2)}) collective-permute-start(bf16[576,768]{1,0:T(8,128)(2,1)} %bitcast.10), channel_id=1, source_target_pairs={{0,1},{3,2},{4,5},{7,6},{8,9},{11,10},{12,13},{15,14},{16,17},{19,... | collective-permute-start | bytes 2654216 | tf_op jit(solution)/shard_map/ppermute | solution.py:1890
  140.0 37.6 %mix_backward.1 = (bf16[576,3072]{1,0:T(8,128)(2,1)}, f32[8,192]{1,0:T(8,128)}, f32[3,128]{1,0:T(4,128)}) custom-call(s32[3]{0:T(128)} %len_ref.5, bf16[192,3072]{1,0:T(8,128)(2,1)} %get-tuple-element.75.grad_ref, bf16[576,3072]{1,0:T(8,128)(2,1)} %get-tuple-element.76.qkv_ref, bf16[192,3072]{1,0:T(8,128)(2,1)} %get-tuple-element.77.first_ref, ...), custom_call_target="tpu_custom_call" | custom-call | flops 20000000000 | bytes 30000000 | tf_op jit(solution)/shard_map/mix_backward/pallas_call | solution.py:670
  177.7 0.0 collective-permute-done.3.we_hbm
  177.7 102.2 %tail.1 = (f32[768,768]{1,0:T(8,128)}, f32[96,768]{1,0:T(8,128)}, f32[768,96]{1,0:T(8,128)}, f32[192,96]{1,0:T(8,128)}, f32[96,576]{1,0:T(8,128)}, /*index=5*/f3...) custom-call(s32[3]{0:T(128)} %len_ref.5, ...), custom_call_target="tpu_custom_call" | custom-call | tf_op jit(solution)/shard_map/tail/pallas_call | solution.py:1374
  279.9 5.2 %settle.1 = (bf16[768,768]{1,0:T(8,128)(2,1)}, f32[768,768]{1,0:T(8,128)}, f32[96,768]{1,0:T(8,128)}, f32[768,96]{1,0:T(8,128)}, f32[192,96]{1,0:T(8,128)}, /*in...) custom-call(bf16[768,768]{1,0:T(8,128)(2,1)} %get-tuple-element.73.r, ...), custom_call_target="tpu_custom_call" | custom-call | tf_op jit(solution)/shard_map/settle/pallas_call | solution.py:1825
  285.1 0.0 copy-start.2
  285.1 1.1 copy.29
  286.3 0.9 copy.30
  287.2 0.0 copy-done.2
  287.2 0.9 copy.31
  (8 shorter events, 0.0 us)
Async XLA Ops:
  0.6 1.0 copy-start
  3.4 38.3 %copy-start.1 = (bf16[224,768]{1,0:T(8,128)(2,1)}, bf16[224,768]{1,0:T(8,128)(2,1)S(1)}, u32[]{:S(2)}) copy-start(bf16[224,768]{1,0:T(8,128)(2,1)S(1)} %fusion.1.own0) | copy-start | bytes 1032196
  3.4 39.1 %collective-permute-start.2 = (bf16[224,768]{1,0:T(8,128)(2,1)S(1)}, bf16[224,768]{1,0:T(8,128)(2,1)S(1)}, u32[]{:S(2)}, u32[]{:S(2)}) collective-permute-start(bf16[224,768]{1,0:T(8,128)(2,1)S(1)} %fusion.1.own0), channel_id=1, source_target_pairs={{0,3},{1,0},{2,1},{3,2},{4,7},{5,4},{6,5},{7,6},{8,11},{9,8},{10,9... | collective-permute-start | bytes 1032200 | tf_op jit(solution)/shard_map/ppermute | solution.py:1875
  8.6 33.9 %collective-permute-start.1 = (bf16[224,768]{1,0:T(8,128)(2,1)S(1)}, bf16[224,768]{1,0:T(8,128)(2,1)S(1)}, u32[]{:S(2)}, u32[]{:S(2)}) collective-permute-start(bf16[224,768]{1,0:T(8,128)(2,1)S(1)} %fusion.1.own0), channel_id=1, source_target_pairs={{0,2},{1,3},{2,0},{3,1},{4,6},{5,7},{6,4},{7,5},{8,10},{9,11},{10,... | collective-permute-start | bytes 1032200 | tf_op jit(solution)/shard_map/ppermute | solution.py:1875
  8.6 33.9 %collective-permute-start = (bf16[224,768]{1,0:T(8,128)(2,1)S(1)}, bf16[224,768]{1,0:T(8,128)(2,1)S(1)}, u32[]{:S(2)}, u32[]{:S(2)}) collective-permute-start(bf16[224,768]{1,0:T(8,128)(2,1)S(1)} %fusion.1.own0), channel_id=1, source_target_pairs={{0,1},{1,2},{2,3},{3,0},{4,5},{5,6},{6,7},{7,4},{8,9},{9,10},{10,1... | collective-permute-start | bytes 1032200 | tf_op jit(solution)/shard_map/ppermute | solution.py:1875
  9.6 32.1 %copy-start.6 = (f32[768]{0:T(1024)S(1)}, f32[768]{0:T(1024)}, u32[]{:S(2)}) copy-start(f32[768]{0:T(1024)} %param.25) | copy-start | bytes 9220
  9.6 32.1 %copy-start.7 = (f32[768]{0:T(1024)S(1)}, f32[768]{0:T(1024)}, u32[]{:S(2)}) copy-start(f32[768]{0:T(1024)} %param.26) | copy-start | bytes 9220
  9.6 32.2 %copy-start.8 = (f32[768]{0:T(1024)S(1)}, f32[768]{0:T(1024)}, u32[]{:S(2)}) copy-start(f32[768]{0:T(1024)} %param.27) | copy-start | bytes 9220
  9.6 32.2 %copy-start.9 = (f32[768]{0:T(1024)S(1)}, f32[768]{0:T(1024)}, u32[]{:S(2)}) copy-start(f32[768]{0:T(1024)} %param.31) | copy-start | bytes 9220
  9.6 32.2 %copy-start.10 = (f32[768]{0:T(1024)S(1)}, f32[768]{0:T(1024)}, u32[]{:S(2)}) copy-start(f32[768]{0:T(1024)} %param.32) | copy-start | bytes 9220
  9.7 32.2 %copy-start.11 = (f32[768]{0:T(1024)S(1)}, f32[768]{0:T(1024)}, u32[]{:S(2)}) copy-start(f32[768]{0:T(1024)} %param.33) | copy-start | bytes 9220
  42.5 0.9 copy-start.3
  42.5 1.0 copy-start.4
  42.6 0.8 copy-start.5
  134.5 43.2 %collective-permute-start.3 = (bf16[576,768]{1,0:T(8,128)(2,1)}, bf16[576,768]{1,0:T(8,128)(2,1)}, u32[]{:S(2)}, u32[]{:S(2)}) collective-permute-start(bf16[576,768]{1,0:T(8,128)(2,1)} %bitcast.10), channel_id=1, source_target_pairs={{0,1},{3,2},{4,5},{7,6},{8,9},{11,10},{12,13},{15,14},{16,17},{19,... | collective-permute-start | bytes 2654216 | tf_op jit(solution)/shard_map/ppermute | solution.py:1890
  285.1 2.0 copy-start.2
where the time goes:
time: 288 us
  Pallas kernels  268 us (93%)
  starting transfers between devices  11.7 us (4%)
  local copies, waits for them, and re-layouts  6.28 us (2%)
    pallas_call x1, Pallas kernels, tail(): pl.pallas_call(tail_kernel, out_shape=[own(quarter, model), own(ff, model...  102 us
    pallas_call x1, Pallas kernels, ffn_middle(): pl.pallas_call(partial(middle_kernel, share), out_shape=[shape(*x) for x...  91 us
    pallas_call x1, Pallas kernels, mix_backward(): pl.pallas_call(partial(mix_backward_kernel, slots, marks, taps), out_shap...  37.6 us
    pallas_call x1, Pallas kernels, mix_forward(): pl.pallas_call(partial(mix_forward_kernel, slots, marks, taps), out_shape...  32.1 us
    ppermute x3, starting transfers between devices, slice_body(): lax.ppermute(pack, 'heads', [(n, (n + i) % 4) for n in range(4)])  6.2 us
  transfers between devices with their start and end apart: 4, of which 0 were waited for; matrix products, arithmetic and copies ran while one was open for 0% of the time, Pallas kernels for 24%

commit v1 on v0

--- a/solution.py
+++ b/solution.py
@@ -58,22 +58,28 @@
     return out
 
 
-def pack_mul(left, right, blocks):
-    left_high, left_low = split(left)
-    right_high, right_low = split(right)
-    right_high, right_low = spread_low(right_high, blocks), spread_low(right_low, blocks)
-    return mul(left_high, right_high) + (mul(left_high, right_low) + mul(left_low, right_high))
-
-
-def pack_mul_t(left, right, blocks):
-    left_high, left_low = split(left)
-    right_high, right_low = split(right)
-    right_high, right_low = spread_low(right_high, blocks), spread_low(right_low, blocks)
-    return mul_t(left_high, right_high) + (mul_t(left_high, right_low) + mul_t(left_low, right_high))
-
-
-def spread_low(x, blocks):
-    return spread(x.astype(f32), blocks).astype(low)
+def ready(x, ones):
+    count = ones.shape[0] // HEAD_DIM
+    high, rest = split(x)
+    return [jnp.concatenate([part] * count, axis=0) * ones for part in (high, rest)]
+
+
+def pack_mul(lefts, right, form=mul):
+    halves = [split(x) for x in lefts]
+    high = [x[0] for x in halves]
+    count = len(lefts)
+    both_parts = form(jnp.concatenate(high + [x[1] for x in halves], axis=0), right[0])
+    rest = form(jnp.concatenate(high, axis=0), right[1])
+    out = []
+    for n in range(count):
+        at = slice(n * HEAD_DIM, (n + 1) * HEAD_DIM)
+        more = slice((count + n) * HEAD_DIM, (count + n + 1) * HEAD_DIM)
+        out.append(both_parts[at] + (both_parts[more] + rest[at]))
+    return out
+
+
+def block_ones(size):
+    return jnp.where(block_grid(size, size), 1.0, 0.0).astype(low)
 
 
 def slot_bounds(len_ref, s, slots):
@@ -172,6 +178,7 @@
         mark_ref[...] = mark_ref[...] * inv_count
         head_blocks = block_grid(width, width)
         slot_blocks = block_grid(packed, packed)
+        ones = block_ones(packed)
         eye = eye_pack(packed)
         scale = HEAD_DIM ** -0.5
 
@@ -195,33 +202,30 @@
             middle_ref[h] = middle
             middles.append(middle)
             inverses_t.append(middle / bound)
-            products.append(pack_mul_t(middle, middle, slot_blocks) / bound)
+            products.append(pack_mul([middle], ready(middle, ones), mul_t)[0] / bound)
         bound_ref[...] = jnp.broadcast_to(bound_total, bound_ref.shape)
 
         def newton(n, carry):
             out = []
             for h in range(heads):
-                inverse_t, product = carry[h]
-                square = pack_mul(product, product, slot_blocks)
-                cube = pack_mul(product, square, slot_blocks)
-                fourth = pack_mul(square, square, slot_blocks)
-                second = 15.0 * eye - 7.0 * product + square
+                before_t, weight, product = carry[h]
+                (inverse_t,) = pack_mul([0.25 * weight], ready(before_t, ones))
+                (square,) = pack_mul([product], ready(product, ones))
+                cube, fourth = pack_mul([product, square], ready(square, ones))
                 third = 13.0 * eye - 15.0 * product + 7.0 * square - cube
                 steps_ref[n, 0, h] = product
-                steps_ref[n, 1, h] = second
+                steps_ref[n, 1, h] = square
                 steps_ref[n, 2, h] = third
                 steps_ref[n, 3, h] = inverse_t
-                out.append(
-                    (
-                        0.25 * pack_mul(third, inverse_t, slot_blocks),
-                        0.25 * (13.0 * product - 15.0 * square + 7.0 * cube - fourth),
-                    )
-                )
+                after = 0.25 * (13.0 * product - 15.0 * square + 7.0 * cube - fourth)
+                out.append((inverse_t, third, after))
             return tuple(out)
 
-        final = lax.fori_loop(0, PINV_ITERS, newton, tuple(zip(inverses_t, products)))
+        start = tuple((x, 4.0 * eye, p) for x, p in zip(inverses_t, products))
+        final = lax.fori_loop(0, PINV_ITERS, newton, start)
         for h in range(heads):
-            inverse_ref[h] = final[h][0]
+            inverse_t, third, _ = final[h]
+            inverse_ref[h] = pack_mul([0.25 * third], ready(inverse_t, ones))[0]
 
         def one_slot(s, _):
             start, end = slot_bounds(len_ref, s, slots)
@@ -280,7 +284,7 @@
         lane_head = lax.broadcasted_iota(jnp.int32, (1, width), 1) // HEAD_DIM
         inner = jnp.zeros((packed, width), f32)
         for h in range(heads):
-            inverse = pack_mul_t(eye, final[h][0], slot_blocks)
+            (inverse,) = pack_mul([eye], ready(inverse_ref[h], ones), mul_t)
             own_values = jnp.where(lane_head == h, value_ref[...], 0.0)
             inner = inner + wide(mul, spread(inverse, slot_blocks), own_values)
         inner_ref[...] = inner
@@ -355,6 +359,7 @@
     scale = HEAD_DIM ** -0.5
     head_blocks = block_grid(width, width)
     slot_blocks = block_grid(packed, packed)
+    ones = block_ones(packed)
     eye = eye_pack(packed)
     count = TILE // SUB
 
@@ -442,45 +447,51 @@
         d_inverses.append(fold(wide(mul_t, own, value_ref[...]), slot_blocks))
     d_value[...] = value_total
 
-    middles_t = [pack_mul_t(eye, middle_ref[h], slot_blocks) for h in range(heads)]
+    def before(n, h, d_inverse):
+        third, inverse_t = steps_ref[n, 2, h], steps_ref[n, 3, h]
+        (d_third,) = pack_mul([0.25 * inverse_t], ready(d_inverse, ones))
+        (earlier,) = pack_mul([0.25 * d_inverse], ready(third, ones))
+        return earlier, d_third
 
     def newton(k, carry):
         n = PINV_ITERS - 1 - k
         out = []
         for h in range(heads):
-            d_inverse, d_middle = carry[h]
-            product = steps_ref[n, 0, h]
-            second = steps_ref[n, 1, h]
-            third = steps_ref[n, 2, h]
-            inverse_t = steps_ref[n, 3, h]
-            middle_t = middles_t[h]
-            d_third = 0.25 * pack_mul(inverse_t, d_inverse, slot_blocks)
-            d_second = -pack_mul(product, d_third, slot_blocks)
-            d_first = -pack_mul(product, d_second, slot_blocks)
+            d_inverse, d_third, grad = carry[h]
+            product, square, third = [steps_ref[n, i, h] for i in range(3)]
+            mixed = 7.0 * product - square
+            by_third, by_one, by_two = pack_mul([third, product, square], ready(grad, ones))
+            left_mixed, left_one = pack_mul([mixed, product], ready(d_third, ones))
+            (right,) = pack_mul([grad], ready(third, ones))
+            (more,) = pack_mul([0.25 * by_one + d_third], ready(mixed, ones))
+            (less,) = pack_mul([0.25 * by_two + left_one], ready(product, ones))
             d_product = (
-                -pack_mul(d_third, second, slot_blocks)
-                - pack_mul(d_second, 7.0 * eye - product, slot_blocks)
-                - d_first
+                0.25 * (right + by_third - 13.0 * grad) - 15.0 * d_third + left_mixed + more - less
             )
-            d_middle = d_middle + pack_mul(d_product, inverse_t, slot_blocks)
-            d_inverse = 0.25 * pack_mul(d_inverse, third, slot_blocks) + pack_mul(
-                middle_t, d_product, slot_blocks
-            )
-            out.append((d_inverse, d_middle))
+            earlier, d_before = before(jnp.maximum(n - 1, 0), h, d_inverse)
+            last = n == 0
+            out.append((jnp.where(last, d_inverse, earlier), d_before, d_product))
         return tuple(out)
 
     zero = jnp.zeros((HEAD_DIM, packed), f32)
-    final = lax.fori_loop(0, PINV_ITERS, newton, tuple((x, zero) for x in d_inverses))
+    start = []
+    for h in range(heads):
+        start.append(before(PINV_ITERS - 1, h, d_inverses[h]) + (zero,))
+    final = lax.fori_loop(0, PINV_ITERS, newton, tuple(start))
     lane_slot = lax.broadcasted_iota(jnp.int32, (1, packed), 1) // marks
     dq_total = jnp.zeros((packed, width), f32)
     dk_total = jnp.zeros((packed, width), f32)
     for h in range(heads):
-        d_inverse, d_middle = final[h]
+        d_inverse, _, d_product = final[h]
         middle = middle_ref[h]
         first_t = steps_ref[0, 3, h]
-        d_inverse_t = pack_mul_t(eye, d_inverse, slot_blocks)
+        (d_inverse_t,) = pack_mul([eye], ready(d_inverse, ones), mul_t)
+        (d_product_t,) = pack_mul([eye], ready(d_product, ones), mul_t)
+        (d_middle,) = pack_mul([d_product + d_product_t], ready(middle, ones))
         col_sums = jnp.sum(middle, axis=0, keepdims=True)
-        share = jnp.sum(d_inverse_t * first_t, axis=0, keepdims=True)
+        share = jnp.sum(
+            d_inverse_t * first_t + d_product * steps_ref[0, 0, h], axis=0, keepdims=True
+        )
         bound = jnp.zeros((1, packed), f32)
         d_bound = jnp.zeros((1, packed), f32)
         hits = jnp.zeros((1, packed), f32)
@@ -494,7 +505,7 @@
             bound = jnp.where(mine, top, bound)
             d_bound = jnp.where(mine, -total / top, d_bound)
             hits = jnp.where(mine, number, hits)
-        d_middle = d_middle + d_inverse_t / bound
+        d_middle = (d_middle + d_inverse_t) / bound
         d_middle = d_middle + jnp.where(col_sums == bound, d_bound / hits, 0.0)
         prod = spread(middle * d_middle, slot_blocks)
         d_sim = prod - spread(middle, slot_blocks) * jnp.sum(prod, axis=1, keepdims=True)
@@ -1164,7 +1175,9 @@
         remote(ref, ref, x_send.at[n, 2], x_recv.at[n, 2], (other, z)).wait_recv()
         own = ones[n][0].astype(f32) + cores[n][0].astype(f32)
         if n == 3:
-            qkvw_own[...] = twos[n][...].astype(f32) + own
+            own = twos[n][...].astype(f32) + own
+            for i in range(3):
+                qkvw_own[i] = own[:, i * width : (i + 1) * width]
             return
         twos[n][...] = (twos[n][...].astype(f32) + own).astype(low)
 
@@ -1194,7 +1207,7 @@
     def end_event(n):
         def write(value):
             out = (down_own, up_own, outw_own)[n]
-            out[...] = jnp.transpose(value) if n > 0 else value
+            out[...] = jnp.transpose(value) if n == 2 else value
 
         @pl.when(is_end)
         def _():
@@ -1374,7 +1387,7 @@
     return pl.pallas_call(
         tail_kernel,
         out_shape=[
-            own(quarter, model), own(ff, model), own(model, ff), own(oh, on), own(qn, qh),
+            own(quarter, model), own(ff, model), own(ff, model), own(oh, on), own(3, qn, width),
             own(1, ff), own(6, model // 32), own(2, width), own(heads, taps), own(1, 1),
         ],
         in_specs=[pl.BlockSpec(memory_space=pltpu.SMEM)]
@@ -1433,14 +1446,14 @@
 
 def middle_kernel(
     share,
-    mixed_ref, own0, own1, own2, own3, tok_hbm, cot_hbm,
+    mixed_ref, own0, own1, own2, own3, tok_hbm, cot_hbm, weight_hbm,
     vec_ref,
     out_hbm, first_hbm, attn_hbm, hidden_hbm, pre_hbm, norm_hbm, ffn_hbm, all_ref, grad_ref,
-    sums_ref, bin_ref,
+    sums_ref, bin_ref, end_hbm,
     out_ref, first_ref, attn_ref, hidden_ref, pre_ref, norm_ref, ffn_ref, tok_ref, cot_ref,
     packs, wof, wo, slope, total, n1_ref, scale_ref, turned,
     a_send, a_recv, f_send, f_recv, s_send, s_recv, p_send, p_recv, g_send, g_recv,
-    own_sem, own_turn, out_sem,
+    own_sem, own_turn, out_sem, w_send, w_recv,
 ):
     b, z, bc, bx, by = place()
     both = bx + by - b
@@ -1551,6 +1564,15 @@
             copy = mix_copy(r, i)
             copy.start()
             issued.append(copy)
+    is_end = (z == 0) | (z == 3)
+    end_copy = remote(
+        weight_hbm, end_hbm, w_send.at[0], w_recv.at[0], (b, jnp.where(z < 2, 1, 2))
+    )
+
+    @pl.when(is_end)
+    def _():
+        end_copy.start()
+
     for copy in local:
         copy.wait()
     for n in range(count):
@@ -1754,6 +1776,17 @@
         return 0
 
     lax.fori_loop(0, tiles, finish, 0)
+
+    @pl.when(is_end)
+    def _():
+        end_copy.wait_send()
+
+    @pl.when(jnp.logical_not(is_end))
+    def _():
+        remote(
+            end_hbm, end_hbm, w_send.at[0], w_recv.at[0], (b, jnp.where(z < 2, 0, 3))
+        ).wait_recv()
+
     for n in range(count):
         corner(n).wait_send()
         for slot, who in enumerate((b, bx, by, both)):
@@ -1762,7 +1795,7 @@
         copy.wait_send()
 
 
-def ffn_middle(mixed_t, packs, tokens, cot, vectors, ff, share):
+def ffn_middle(mixed_t, packs, tokens, cot, weight_t, vectors, ff, share):
     width, tok_count = mixed_t.shape
     quarter, model = tok_count // 4, tokens.shape[1]
     size = quarter // 3
@@ -1788,9 +1821,10 @@
             shape((width, tok_count), low),
             shape((8, model), f32),
             shape((8, 32 * ff), f32),
+            shape(weight_t.shape, low),
         ],
-        in_specs=[hbm] + [vmem] * 4 + [hbm] * 2 + [vmem],
-        out_specs=[hbm] * 7 + [vmem, hbm, vmem, vmem],
+        in_specs=[hbm] + [vmem] * 4 + [hbm] * 3 + [vmem],
+        out_specs=[hbm] * 7 + [vmem, hbm, vmem, vmem, hbm],
         scratch_shapes=[pltpu.VMEM(*x) for x in kept]
         + [
             pltpu.VMEM((quarter, model), low),
@@ -1805,13 +1839,13 @@
             pltpu.VMEM((3, 4 * width, size), low),
             dma((3, 3)), dma((3, 3)), dma((4, 2, 4)), dma((4, 2, 4)), dma((4,)), dma((4,)),
             dma((4, 4)), dma((4, 4)), dma((3, 3)), dma((3, 3)),
-            dma((7,)), dma((3,)), dma((3, 7)),
+            dma((7,)), dma((3,)), dma((3, 7)), dma((1,)), dma((1,)),
         ],
         compiler_params=pltpu.CompilerParams(
             collective_id=1, has_side_effects=True, vmem_limit_bytes=63 * 1024 * 1024
         ),
         name="middle",
-    )(mixed_t, *packs, tokens, cot, vectors)
+    )(mixed_t, *packs, tokens, cot, weight_t, vectors)
 
 
 def settle_kernel(*refs):
@@ -1821,12 +1855,20 @@
 
 
 def settle(*arrays):
-    vmem = pl.BlockSpec(memory_space=pltpu.VMEM)
+    steps = 4
+    tall = arrays[0].shape[0]
+
+    def spec(x):
+        if x.shape[0] == tall:
+            return pl.BlockSpec((tall // steps, *x.shape[1:]), lambda n: (n, 0))
+        return pl.BlockSpec(x.shape, lambda n: (0,) * x.ndim)
+
     return pl.pallas_call(
         settle_kernel,
+        grid=(steps,),
         out_shape=[jax.ShapeDtypeStruct(x.shape, x.dtype) for x in arrays],
-        in_specs=[vmem] * len(arrays),
-        out_specs=[vmem] * len(arrays),
+        in_specs=[spec(x) for x in arrays],
+        out_specs=[spec(x) for x in arrays],
         name="settle",
     )(*arrays)
 
@@ -1883,11 +1925,9 @@
     )
     (
         final_low, grad_first, grad_attn_low, hidden_low, grad_pre, norm1_low, grad_ffn_low,
-        mixed_all, grad_mix_t, vector_sums, bias_sums,
-    ) = ffn_middle(mixed_t, packs, tokens, cotangent, vectors, ff_own, share)
+        mixed_all, grad_mix_t, vector_sums, bias_sums, weight_end,
+    ) = ffn_middle(mixed_t, packs, tokens, cotangent, weight_t, vectors, ff_own, share)
     saved = (qkv_t, first, last, mark, value, inner, denom, middle, steps, inverse)
-    held, grad_mix_t = lax.optimization_barrier((weight_t, grad_mix_t))
-    weight_end = lax.ppermute(held, "heads", [(0, 1), (3, 2)])
     grad_t, grad_bias, grad_conv = mix_backward(
         seq_lengths, grad_mix_t, saved, conv_weight, slots, marks
     )
@@ -1909,11 +1949,11 @@
     return (
         final_low,
         input_grad,
-        qkv_share.reshape(model // 8, 3, width),
+        jnp.swapaxes(qkv_share, 0, 1),
         bias_out,
         conv_out,
         out_share,
-        up_share,
+        jnp.transpose(up_share),
         in_bias_share.reshape(ff_own),
         down_share,
         vector_share,

time: 288 us -> 278 us (0.965)
  starting transfers between devices: 11.7 us -> 6.2 us
  Pallas kernels: 268 us -> 264 us
    pallas_call x1, Pallas kernels: 37.6 us -> 32.1 us  [mix_backward(): pl.pallas_call(partial(mix_backward_kernel, slots, marks, taps), out_shap...]
    ppermute x1 -> x0, starting transfers between devices: 5.51 us -> none  [slice_body(): weight_end = lax.ppermute(held, 'heads', [(0, 1), (3, 2)])]
  transfers between devices with their start and end apart: 4 -> 3, of which waited for: 0 -> 0; matrix products, arithmetic and copies ran while one was open for 0% -> 0% of each run, Pallas kernels for 24% -> 11%
where the time goes in v1:
time: 278 us; the launch traced here: 276 us
  Pallas kernels  264 us (95%)
  starting transfers between devices  6.2 us (2%)
  local copies, waits for them, and re-layouts  3.91 us (1%)
    pallas_call x1, Pallas kernels, tail(): pl.pallas_call(tail_kernel, out_shape=[own(quarter, model), own(ff, model...  104 us
    pallas_call x1, Pallas kernels, ffn_middle(): pl.pallas_call(partial(middle_kernel, share), out_shape=[shape(*x) for x...  91 us
    pallas_call x1, Pallas kernels, mix_backward(): pl.pallas_call(partial(mix_backward_kernel, slots, marks, taps), out_shap...  32.1 us
    pallas_call x1, Pallas kernels, mix_forward(): pl.pallas_call(partial(mix_forward_kernel, slots, marks, taps), out_shape...  30.9 us
    ppermute x3, starting transfers between devices, slice_body(): lax.ppermute(pack, 'heads', [(n, (n + i) % 4) for n in range(4)])  6.2 us
    pallas_call x1, Pallas kernels, settle(): pl.pallas_call(settle_kernel, grid=(steps,), out_shape=[jax.ShapeDtypeStr...  5.71 us
  transfers between devices with their start and end apart: 3, of which 0 were waited for; matrix products, arithmetic and copies ran while one was open for 0% of the time, Pallas kernels for 11%

profile of v1, /device:TPU:0, one launch (start us, length us, event | category | flops | bytes accessed | tf_op | source)
XLA Modules:
  0.0 276.0 jit_solution(2055008506358244446)
XLA Ops:
  0.6 0.0 copy-start
  0.7 0.9 copy-done
  1.6 0.8 dynamic_update_slice.6
  2.4 1.0 fusion.1.own0
  3.4 0.0 copy-start.1
  3.4 5.2 %collective-permute-start.2 = (bf16[224,768]{1,0:T(8,128)(2,1)S(1)}, bf16[224,768]{1,0:T(8,128)(2,1)S(1)}, u32[]{:S(2)}, u32[]{:S(2)}) collective-permute-start(bf16[224,768]{1,0:T(8,128)(2,1)S(1)} %fusion.1.own0), channel_id=1, source_target_pairs={{0,3},{1,0},{2,1},{3,2},{4,7},{5,4},{6,5},{7,6},{8,11},{9,8},{10,9... | collective-permute-start | bytes 1032200 | tf_op jit(solution)/shard_map/ppermute | solution.py:1917
  8.6 0.0 collective-permute-start.1
  8.6 1.0 collective-permute-start
  9.6 0.0 copy-start.5
  9.6 0.0 copy-start.6
  9.6 0.0 copy-start.7
  9.6 0.0 copy-start.8
  9.6 0.0 copy-start.9
  9.7 0.0 copy-start.10
  9.7 30.9 %mix_forward.1 = (bf16[576,3072]{1,0:T(8,128)(2,1)}, bf16[192,3072]{1,0:T(8,128)(2,1)}, bf16[192,3072]{1,0:T(8,128)(2,1)}, bf16[192,3072]{1,0:T(8,128)(2,1)}, f3...) custom-call(s32[3]{0:T(128)} %len_ref.5, ...), custom_call_target="tpu_custom_call" | custom-call | flops 20000000000 | bytes 30000000 | tf_op jit(solution)/shard_map/mix_forward/pallas_call | solution.py:640
  40.6 0.0 copy-done.1
  40.6 0.0 copy-done.5
  40.6 0.0 copy-done.6
  40.6 0.0 copy-done.7
  40.6 0.0 copy-done.8
  40.7 0.0 copy-done.9
  40.7 0.0 copy-done.10
  40.7 0.6 stack.27.vec_ref
  41.3 0.0 collective-permute-done.2.own3
  41.3 0.0 copy-start.2
  41.4 0.0 collective-permute-done.1.own2
  41.4 0.0 copy-start.3
  41.4 0.0 collective-permute-done.own1
  41.4 0.7 copy-done.3
  42.1 0.0 copy-start.4
  42.1 0.7 copy-done.4
  42.8 0.0 copy-done.2
  42.8 91.0 %middle.1 = (bf16[768,768]{1,0:T(8,128)(2,1)}, f32[768,768]{1,0:T(8,128)}, bf16[768,768]{1,0:T(8,128)(2,1)}, bf16[768,3072]{1,0:T(8,128)(2,1)}, bf16[768,3072]{1...) custom-call(bf16[192,3072]{1,0:T(8,128)(2,1)} %get-tuple-element.71., ...), custom_call_target="tpu_custom_call" | custom-call | tf_op jit(solution)/shard_map/middle/pallas_call | solution.py:1816
  133.8 32.1 %mix_backward.1 = (bf16[576,3072]{1,0:T(8,128)(2,1)}, f32[8,192]{1,0:T(8,128)}, f32[3,128]{1,0:T(4,128)}) custom-call(s32[3]{0:T(128)} %len_ref.5, bf16[192,3072]{1,0:T(8,128)(2,1)} %get-tuple-element.73.grad_ref, bf16[576,3072]{1,0:T(8,128)(2,1)} %get-tuple-element.74.qkv_ref, bf16[192,3072]{1,0:T(8,128)(2,1)} %get-tuple-element.75.first_ref, ...), custom_call_target="tpu_custom_call" | custom-call | flops 20000000000 | bytes 30000000 | tf_op jit(solution)/shard_map/mix_backward/pallas_call | solution.py:681
  165.9 104.2 %tail.1 = (f32[768,768]{1,0:T(8,128)}, f32[96,768]{1,0:T(8,128)}, f32[96,768]{1,0:T(8,128)}, f32[192,96]{1,0:T(8,128)}, f32[3,96,192]{2,1,0:T(8,128)}, /*index=5...) custom-call(s32[3]{0:T(128)} %len_ref.5, ...), custom_call_target="tpu_custom_call" | custom-call | tf_op jit(solution)/shard_map/tail/pallas_call | solution.py:1387
  270.2 5.7 %settle.1 = (bf16[768,768]{1,0:T(8,128)(2,1)}, f32[768,768]{1,0:T(8,128)}, f32[96,768]{1,0:T(8,128)}, f32[96,768]{1,0:T(8,128)}, f32[192,96]{1,0:T(8,128)}, /*in...) custom-call(bf16[768,768]{1,0:T(8,128)(2,1)} %get-tuple-element.72.r, ...), custom_call_target="tpu_custom_call" | custom-call | tf_op jit(solution)/shard_map/settle/pallas_call | solution.py:1866
  (8 shorter events, 0.0 us)
Async XLA Ops:
  0.6 1.0 copy-start
  3.4 37.1 %copy-start.1 = (bf16[224,768]{1,0:T(8,128)(2,1)}, bf16[224,768]{1,0:T(8,128)(2,1)S(1)}, u32[]{:S(2)}) copy-start(bf16[224,768]{1,0:T(8,128)(2,1)S(1)} %fusion.1.own0) | copy-start | bytes 1032196
  3.4 37.9 %collective-permute-start.2 = (bf16[224,768]{1,0:T(8,128)(2,1)S(1)}, bf16[224,768]{1,0:T(8,128)(2,1)S(1)}, u32[]{:S(2)}, u32[]{:S(2)}) collective-permute-start(bf16[224,768]{1,0:T(8,128)(2,1)S(1)} %fusion.1.own0), channel_id=1, source_target_pairs={{0,3},{1,0},{2,1},{3,2},{4,7},{5,4},{6,5},{7,6},{8,11},{9,8},{10,9... | collective-permute-start | bytes 1032200 | tf_op jit(solution)/shard_map/ppermute | solution.py:1917
  8.6 32.7 %collective-permute-start.1 = (bf16[224,768]{1,0:T(8,128)(2,1)S(1)}, bf16[224,768]{1,0:T(8,128)(2,1)S(1)}, u32[]{:S(2)}, u32[]{:S(2)}) collective-permute-start(bf16[224,768]{1,0:T(8,128)(2,1)S(1)} %fusion.1.own0), channel_id=1, source_target_pairs={{0,2},{1,3},{2,0},{3,1},{4,6},{5,7},{6,4},{7,5},{8,10},{9,11},{10,... | collective-permute-start | bytes 1032200 | tf_op jit(solution)/shard_map/ppermute | solution.py:1917
  8.6 32.8 %collective-permute-start = (bf16[224,768]{1,0:T(8,128)(2,1)S(1)}, bf16[224,768]{1,0:T(8,128)(2,1)S(1)}, u32[]{:S(2)}, u32[]{:S(2)}) collective-permute-start(bf16[224,768]{1,0:T(8,128)(2,1)S(1)} %fusion.1.own0), channel_id=1, source_target_pairs={{0,1},{1,2},{2,3},{3,0},{4,5},{5,6},{6,7},{7,4},{8,9},{9,10},{10,1... | collective-permute-start | bytes 1032200 | tf_op jit(solution)/shard_map/ppermute | solution.py:1917
  9.6 30.9 %copy-start.5 = (f32[768]{0:T(1024)S(1)}, f32[768]{0:T(1024)}, u32[]{:S(2)}) copy-start(f32[768]{0:T(1024)} %param.25) | copy-start | bytes 9220
  9.6 31.0 %copy-start.6 = (f32[768]{0:T(1024)S(1)}, f32[768]{0:T(1024)}, u32[]{:S(2)}) copy-start(f32[768]{0:T(1024)} %param.26) | copy-start | bytes 9220
  9.6 31.0 %copy-start.7 = (f32[768]{0:T(1024)S(1)}, f32[768]{0:T(1024)}, u32[]{:S(2)}) copy-start(f32[768]{0:T(1024)} %param.27) | copy-start | bytes 9220
  9.6 31.0 %copy-start.8 = (f32[768]{0:T(1024)S(1)}, f32[768]{0:T(1024)}, u32[]{:S(2)}) copy-start(f32[768]{0:T(1024)} %param.31) | copy-start | bytes 9220
  9.6 31.0 %copy-start.9 = (f32[768]{0:T(1024)S(1)}, f32[768]{0:T(1024)}, u32[]{:S(2)}) copy-start(f32[768]{0:T(1024)} %param.32) | copy-start | bytes 9220
  9.7 31.0 %copy-start.10 = (f32[768]{0:T(1024)S(1)}, f32[768]{0:T(1024)}, u32[]{:S(2)}) copy-start(f32[768]{0:T(1024)} %param.33) | copy-start | bytes 9220
  41.3 1.5 copy-start.2
  41.4 0.7 copy-start.3
  42.1 0.7 copy-start.4

commit v2 on v1

--- a/solution.py
+++ b/solution.py
@@ -131,9 +131,10 @@
 def mix_forward_kernel(
     slots, marks, taps,
     len_ref, tok_ref, weight_ref, bias_ref, conv_ref,
-    qkv_ref, first_ref, last_ref, mixed_ref, mark_ref, value_ref, inner_ref,
-    denom_ref, middle_ref, steps_ref, inverse_ref, bound_ref,
-    vpad, scores, vsum, bias_col, conv_own,
+    qkv_hbm, first_hbm, last_hbm, mixed_ref, mark_ref, value_ref, inner_ref,
+    denom_ref, middle_ref, steps_hbm, inverse_ref, bound_ref,
+    qkv_ref, first_ref, last_ref, steps_ref,
+    vpad, scores, vsum, bias_col, conv_own, out_sem,
 ):
     step = pl.program_id(0)
     width = first_ref.shape[0]
@@ -173,8 +174,19 @@
     last_ref[:, pl.ds(at, TILE)] = jnp.zeros((width, TILE), low)
     mixed_ref[:, pl.ds(at, TILE)] = jnp.zeros((width, TILE), low)
 
+    leaving = [
+        pltpu.make_async_copy(src, dst, out_sem.at[n])
+        for n, (src, dst) in enumerate(
+            (
+                (qkv_ref, qkv_hbm), (steps_ref, steps_hbm), (first_ref, first_hbm),
+                (last_ref, last_hbm),
+            )
+        )
+    ]
+
     @pl.when(step == tiles - 1)
     def _():
+        leaving[0].start()
         mark_ref[...] = mark_ref[...] * inv_count
         head_blocks = block_grid(width, width)
         slot_blocks = block_grid(packed, packed)
@@ -226,6 +238,7 @@
         for h in range(heads):
             inverse_t, third, _ = final[h]
             inverse_ref[h] = pack_mul([0.25 * third], ready(inverse_t, ones))[0]
+        leaving[1].start()
 
         def one_slot(s, _):
             start, end = slot_bounds(len_ref, s, slots)
@@ -280,6 +293,8 @@
             return 0
 
         lax.fori_loop(0, slots, one_slot, 0)
+        leaving[2].start()
+        leaving[3].start()
 
         lane_head = lax.broadcasted_iota(jnp.int32, (1, width), 1) // HEAD_DIM
         inner = jnp.zeros((packed, width), f32)
@@ -310,6 +325,8 @@
             return lax.fori_loop(lo, hi, out_tile, 0)
 
         lax.fori_loop(0, slots, out_slot, 0)
+        for copy in leaving:
+            copy.wait()
 
 
 def own_taps(own_ref, all_ref, z):
@@ -347,9 +364,10 @@
 
 def mix_backward_kernel(
     slots, marks, taps,
-    len_ref, grad_ref, qkv_ref, first_ref, last_ref, mark_ref, value_ref, inner_ref,
-    denom_ref, middle_ref, steps_ref, inverse_ref, conv_ref,
-    out_ref, bias_ref, conv_out_ref,
+    len_ref, grad_ref, qkv_ref, first_ref, last_hbm, mark_ref, value_ref, inner_ref,
+    denom_ref, middle_ref, steps_hbm, inverse_ref, conv_ref,
+    out_hbm, bias_ref, conv_out_ref,
+    last_ref, steps_ref, out_ref, move_sem,
     gpad, vpad, ds_first, ds_last, conv_grad, d_inner, d_k, d_q, d_value, conv_own,
 ):
     width = first_ref.shape[0]
@@ -362,6 +380,10 @@
     ones = block_ones(packed)
     eye = eye_pack(packed)
     count = TILE // SUB
+    last_in = pltpu.make_async_copy(last_hbm, last_ref, move_sem.at[0])
+    steps_in = pltpu.make_async_copy(steps_hbm, steps_ref, move_sem.at[1])
+    steps_in.start()
+    last_in.start()
 
     for padded, source in ((gpad, grad_ref[...]), (vpad, qkv_ref[2 * width :, :])):
         padded[:, :SUB] = jnp.zeros((width, SUB), low)
@@ -473,6 +495,7 @@
             out.append((jnp.where(last, d_inverse, earlier), d_before, d_product))
         return tuple(out)
 
+    steps_in.wait()
     zero = jnp.zeros((HEAD_DIM, packed), f32)
     start = []
     for h in range(heads):
@@ -562,7 +585,11 @@
         d_q[own_rows(s), :] += fold(query_total, head_blocks) * scale
         return 0
 
+    last_in.wait()
     lax.fori_loop(0, slots, last_slot, 0)
+    values = pl.ds(2 * width, width)
+    values_out = pltpu.make_async_copy(out_ref.at[values], out_hbm.at[values], move_sem.at[2])
+    values_out.start()
 
     inv_count = slot_marks(len_ref, 0, slots, marks, SUB)[1]
     d_q[...] = d_q[...] * inv_count
@@ -598,6 +625,9 @@
         return lax.fori_loop(lo, hi, tile, 0)
 
     lax.fori_loop(0, slots, final_slot, 0)
+    others = pl.ds(0, 2 * width)
+    others_out = pltpu.make_async_copy(out_ref.at[others], out_hbm.at[others], move_sem.at[3])
+    others_out.start()
 
     def bias_tile(n, carry):
         t = pl.multiple_of(n * TILE, TILE)
@@ -614,6 +644,8 @@
     bias_ref[...] = jnp.zeros_like(bias_ref)
     bias_ref[0:1, :] = jnp.sum(jnp.transpose(q_sum), axis=0, keepdims=True)
     bias_ref[1:2, :] = jnp.sum(jnp.transpose(v_sum), axis=0, keepdims=True)
+    values_out.wait()
+    others_out.wait()
 
 
 def mix_forward(seq_lengths, tokens, weight_t, bias, conv, slots, marks):
@@ -637,6 +669,7 @@
         ((heads, HEAD_DIM, packed), f32),
         ((8, 128), f32),
     ]
+    apart = (0, 1, 2, 9)
     return pl.pallas_call(
         partial(mix_forward_kernel, slots, marks, taps),
         out_shape=[jax.ShapeDtypeStruct(s, t) for s, t in shapes],
@@ -649,13 +682,18 @@
                 whole(*bias.shape),
                 whole(*conv.shape),
             ],
-            out_specs=[whole(*s) for s, _ in shapes],
-            scratch_shapes=[
+            out_specs=[
+                pl.BlockSpec(memory_space=pl.ANY) if n in apart else whole(*s)
+                for n, (s, _) in enumerate(shapes)
+            ],
+            scratch_shapes=[pltpu.VMEM(*shapes[n]) for n in apart]
+            + [
                 pltpu.VMEM((width, tok_count + 2 * SUB), low),
                 pltpu.VMEM((width, tok_count), f32),
                 pltpu.VMEM((8, width), f32),
                 pltpu.VMEM((bias.shape[1], 2 * bias.shape[0]), f32),
                 pltpu.VMEM((heads, taps), f32),
+                pltpu.SemaphoreType.DMA((len(apart),)),
             ],
         ),
         compiler_params=pltpu.CompilerParams(vmem_limit_bytes=56 * 1024 * 1024),
@@ -678,15 +716,20 @@
     )
     shapes = [((3 * width, tok_count), low), ((8, width), f32), ((heads, SUB), f32)]
     square = pltpu.VMEM((packed, width), f32)
+    hbm = pl.BlockSpec(memory_space=pl.ANY)
     return pl.pallas_call(
         partial(mix_backward_kernel, slots, marks, taps),
         out_shape=[jax.ShapeDtypeStruct(s, t) for s, t in shapes],
         grid_spec=pltpu.PrefetchScalarGridSpec(
             num_scalar_prefetch=1,
             grid=(1,),
-            in_specs=[whole(x.shape) for x in args],
-            out_specs=[whole(s) for s, _ in shapes],
+            in_specs=[hbm if n in (3, 9) else whole(x.shape) for n, x in enumerate(args)],
+            out_specs=[hbm] + [whole(s) for s, _ in shapes[1:]],
             scratch_shapes=[
+                pltpu.VMEM(last.shape, low),
+                pltpu.VMEM(steps.shape, f32),
+                pltpu.VMEM(*shapes[0]),
+                pltpu.SemaphoreType.DMA((4,)),
                 pltpu.VMEM((width, tok_count + 2 * SUB), low),
                 pltpu.VMEM((width, tok_count + 2 * SUB), low),
                 pltpu.VMEM((width, tok_count), low),
@@ -1823,7 +1866,7 @@
             shape((8, 32 * ff), f32),
             shape(weight_t.shape, low),
         ],
-        in_specs=[hbm] + [vmem] * 4 + [hbm] * 3 + [vmem],
+        in_specs=[hbm] * 8 + [vmem],
         out_specs=[hbm] * 7 + [vmem, hbm, vmem, vmem, hbm],
         scratch_shapes=[pltpu.VMEM(*x) for x in kept]
         + [
@@ -1848,27 +1891,41 @@
     )(mixed_t, *packs, tokens, cot, weight_t, vectors)
 
 
-def settle_kernel(*refs):
-    count = len(refs) // 2
+def settle_kernel(count, pieces, *refs):
+    sources, results = refs[:count], refs[count : 2 * count]
+    held, came, went = refs[2 * count : 3 * count], refs[3 * count], refs[3 * count + 1]
+    moves = []
     for n in range(count):
-        refs[count + n][...] = refs[n][...]
+        rows = held[n].shape[0] // pieces[n]
+        for k in range(pieces[n]):
+            at = pl.ds(k * rows, rows)
+            moves.append((sources[n].at[at], held[n].at[at], results[n].at[at]))
+    coming = [
+        pltpu.make_async_copy(src, mid, came.at[n]) for n, (src, mid, _) in enumerate(moves)
+    ]
+    going = [
+        pltpu.make_async_copy(mid, dst, went.at[n]) for n, (_, mid, dst) in enumerate(moves)
+    ]
+    for copy in coming:
+        copy.start()
+    for arrival, copy in zip(coming, going):
+        arrival.wait()
+        copy.start()
+    for copy in going:
+        copy.wait()
 
 
 def settle(*arrays):
-    steps = 4
-    tall = arrays[0].shape[0]
-
-    def spec(x):
-        if x.shape[0] == tall:
-            return pl.BlockSpec((tall // steps, *x.shape[1:]), lambda n: (n, 0))
-        return pl.BlockSpec(x.shape, lambda n: (0,) * x.ndim)
-
+    count = len(arrays)
+    pieces = [4 if x.size > 2**18 else 1 for x in arrays]
+    hbm = pl.BlockSpec(memory_space=pl.ANY)
     return pl.pallas_call(
-        settle_kernel,
-        grid=(steps,),
+        partial(settle_kernel, count, pieces),
         out_shape=[jax.ShapeDtypeStruct(x.shape, x.dtype) for x in arrays],
-        in_specs=[spec(x) for x in arrays],
-        out_specs=[spec(x) for x in arrays],
+        in_specs=[hbm] * count,
+        out_specs=[hbm] * count,
+        scratch_shapes=[pltpu.VMEM(x.shape, x.dtype) for x in arrays]
+        + [pltpu.SemaphoreType.DMA((sum(pieces),))] * 2,
         name="settle",
     )(*arrays)
 

time: 278 us -> 272 us (0.978)
  Pallas kernels: 264 us -> 257 us
    pallas_call x1, Pallas kernels: 30.9 us -> 27.4 us  [mix_forward(): pl.pallas_call(partial(mix_forward_kernel, slots, marks, taps), out_shape...]
  transfers between devices with their start and end apart: 3 -> 3, of which waited for: 0 -> 1; matrix products, arithmetic and copies ran while one was open for 0% -> 0% of each run, Pallas kernels for 11% -> 10%
where the time goes in v2:
time: 272 us; the launch traced here: 270 us
  Pallas kernels  257 us (94%)
  starting transfers between devices  6.2 us (2%)
  local copies, waits for them, and re-layouts  3.96 us (1%)
    pallas_call x1, Pallas kernels, tail(): pl.pallas_call(tail_kernel, out_shape=[own(quarter, model), own(ff, model...  104 us
    pallas_call x1, Pallas kernels, ffn_middle(): pl.pallas_call(partial(middle_kernel, share), out_shape=[shape(*x) for x...  90.3 us
    pallas_call x1, Pallas kernels, mix_backward(): pl.pallas_call(partial(mix_backward_kernel, slots, marks, taps), out_shap...  30.2 us
    pallas_call x1, Pallas kernels, mix_forward(): pl.pallas_call(partial(mix_forward_kernel, slots, marks, taps), out_shape...  27.4 us
    ppermute x3, starting transfers between devices, slice_body(): lax.ppermute(pack, 'heads', [(n, (n + i) % 4) for n in range(4)])  6.2 us
  transfers between devices with their start and end apart: 3, of which 1 were waited for; matrix products, arithmetic and copies ran while one was open for 0% of the time, Pallas kernels for 10%

profile of v2, /device:TPU:0, one launch (start us, length us, event | category | flops | bytes accessed | tf_op | source)
XLA Modules:
  0.0 269.5 jit_solution(12330134910365058347)
XLA Ops:
  0.6 0.0 copy-start
  0.7 0.9 copy-done
  1.6 0.8 dynamic_update_slice.6
  2.4 1.0 fusion.1.own0
  3.4 0.0 copy-start.1
  3.4 5.2 %collective-permute-start.2 = (bf16[224,768]{1,0:T(8,128)(2,1)S(1)}, bf16[224,768]{1,0:T(8,128)(2,1)S(1)}, u32[]{:S(2)}, u32[]{:S(2)}) collective-permute-start(bf16[224,768]{1,0:T(8,128)(2,1)S(1)} %fusion.1.own0), channel_id=1, source_target_pairs={{0,3},{1,0},{2,1},{3,2},{4,7},{5,4},{6,5},{7,6},{8,11},{9,8},{10,9... | collective-permute-start | bytes 1032200 | tf_op jit(solution)/shard_map/ppermute | solution.py:1974
  8.6 0.0 collective-permute-start.1
  8.6 1.0 collective-permute-start
  9.6 0.0 copy-start.5
  9.6 0.0 copy-start.6
  9.6 0.0 copy-start.7
  9.6 0.0 copy-start.8
  9.6 0.0 copy-start.9
  9.7 0.0 copy-start.10
  9.7 27.4 %mix_forward.1 = (bf16[576,3072]{1,0:T(8,128)(2,1)}, bf16[192,3072]{1,0:T(8,128)(2,1)}, bf16[192,3072]{1,0:T(8,128)(2,1)}, bf16[192,3072]{1,0:T(8,128)(2,1)}, f3...) custom-call(s32[3]{0:T(128)} %len_ref.5, ...), custom_call_target="tpu_custom_call" | custom-call | flops 20000000000 | bytes 30000000 | tf_op jit(solution)/shard_map/mix_forward/pallas_call | solution.py:673
  37.1 0.0 copy-done.1
  37.1 0.0 copy-done.5
  37.1 0.0 copy-done.6
  37.2 0.0 copy-done.7
  37.2 0.0 copy-done.8
  37.2 0.0 copy-done.9
  37.2 0.0 copy-done.10
  37.2 0.6 stack.27.vec_ref
  37.9 0.0 collective-permute-done.2.own3
  37.9 0.0 copy-start.2
  37.9 0.1 collective-permute-done.1.own2
  38.0 0.0 copy-start.3
  38.0 0.0 collective-permute-done.own1
  38.0 0.8 copy-done.3
  38.7 0.0 copy-start.4
  38.7 0.7 copy-done.4
  39.5 0.0 copy-done.2
  39.5 90.3 %middle.1 = (bf16[768,768]{1,0:T(8,128)(2,1)}, f32[768,768]{1,0:T(8,128)}, bf16[768,768]{1,0:T(8,128)(2,1)}, bf16[768,3072]{1,0:T(8,128)(2,1)}, bf16[768,3072]{1...) custom-call(bf16[192,3072]{1,0:T(8,128)(2,1)} %get-tuple-element.71., ...), custom_call_target="tpu_custom_call" | custom-call | tf_op jit(solution)/shard_map/middle/pallas_call | solution.py:1859
  129.8 30.2 %mix_backward.1 = (bf16[576,3072]{1,0:T(8,128)(2,1)}, f32[8,192]{1,0:T(8,128)}, f32[3,128]{1,0:T(4,128)}) custom-call(s32[3]{0:T(128)} %len_ref.5, bf16[192,3072]{1,0:T(8,128)(2,1)} %get-tuple-element.73.grad_ref, bf16[576,3072]{1,0:T(8,128)(2,1)} %get-tuple-element.74.qkv_ref, bf16[192,3072]{1,0:T(8,128)(2,1)} %get-tuple-element.75.first_ref, ...), custom_call_target="tpu_custom_call" | custom-call | flops 20000000000 | bytes 30000000 | tf_op jit(solution)/shard_map/mix_backward/pallas_call | solution.py:720
  160.0 104.5 %tail.1 = (f32[768,768]{1,0:T(8,128)}, f32[96,768]{1,0:T(8,128)}, f32[96,768]{1,0:T(8,128)}, f32[192,96]{1,0:T(8,128)}, f32[3,96,192]{2,1,0:T(8,128)}, /*index=5...) custom-call(s32[3]{0:T(128)} %len_ref.5, ...), custom_call_target="tpu_custom_call" | custom-call | tf_op jit(solution)/shard_map/tail/pallas_call | solution.py:1430
  264.5 4.8 %settle.1 = (bf16[768,768]{1,0:T(8,128)(2,1)}, f32[768,768]{1,0:T(8,128)}, f32[96,768]{1,0:T(8,128)}, f32[96,768]{1,0:T(8,128)}, f32[192,96]{1,0:T(8,128)}, /*in...) custom-call(bf16[768,768]{1,0:T(8,128)(2,1)} %get-tuple-element.72.r, ...), custom_call_target="tpu_custom_call" | custom-call | tf_op jit(solution)/shard_map/settle/pallas_call | solution.py:1922
  (8 shorter events, 0.0 us)
Async XLA Ops:
  0.6 1.0 copy-start
  3.4 33.7 %copy-start.1 = (bf16[224,768]{1,0:T(8,128)(2,1)}, bf16[224,768]{1,0:T(8,128)(2,1)S(1)}, u32[]{:S(2)}) copy-start(bf16[224,768]{1,0:T(8,128)(2,1)S(1)} %fusion.1.own0) | copy-start | bytes 1032196
  3.4 34.5 %collective-permute-start.2 = (bf16[224,768]{1,0:T(8,128)(2,1)S(1)}, bf16[224,768]{1,0:T(8,128)(2,1)S(1)}, u32[]{:S(2)}, u32[]{:S(2)}) collective-permute-start(bf16[224,768]{1,0:T(8,128)(2,1)S(1)} %fusion.1.own0), channel_id=1, source_target_pairs={{0,3},{1,0},{2,1},{3,2},{4,7},{5,4},{6,5},{7,6},{8,11},{9,8},{10,9... | collective-permute-start | bytes 1032200 | tf_op jit(solution)/shard_map/ppermute | solution.py:1974
  8.6 29.3 %collective-permute-start.1 = (bf16[224,768]{1,0:T(8,128)(2,1)S(1)}, bf16[224,768]{1,0:T(8,128)(2,1)S(1)}, u32[]{:S(2)}, u32[]{:S(2)}) collective-permute-start(bf16[224,768]{1,0:T(8,128)(2,1)S(1)} %fusion.1.own0), channel_id=1, source_target_pairs={{0,2},{1,3},{2,0},{3,1},{4,6},{5,7},{6,4},{7,5},{8,10},{9,11},{10,... | collective-permute-start | bytes 1032200 | tf_op jit(solution)/shard_map/ppermute | solution.py:1974
  8.6 29.3 %collective-permute-start = (bf16[224,768]{1,0:T(8,128)(2,1)S(1)}, bf16[224,768]{1,0:T(8,128)(2,1)S(1)}, u32[]{:S(2)}, u32[]{:S(2)}) collective-permute-start(bf16[224,768]{1,0:T(8,128)(2,1)S(1)} %fusion.1.own0), channel_id=1, source_target_pairs={{0,1},{1,2},{2,3},{3,0},{4,5},{5,6},{6,7},{7,4},{8,9},{9,10},{10,1... | collective-permute-start | bytes 1032200 | tf_op jit(solution)/shard_map/ppermute | solution.py:1974
  9.6 27.5 %copy-start.5 = (f32[768]{0:T(1024)S(1)}, f32[768]{0:T(1024)}, u32[]{:S(2)}) copy-start(f32[768]{0:T(1024)} %param.25) | copy-start | bytes 9220
  9.6 27.5 %copy-start.6 = (f32[768]{0:T(1024)S(1)}, f32[768]{0:T(1024)}, u32[]{:S(2)}) copy-start(f32[768]{0:T(1024)} %param.26) | copy-start | bytes 9220
  9.6 27.5 %copy-start.7 = (f32[768]{0:T(1024)S(1)}, f32[768]{0:T(1024)}, u32[]{:S(2)}) copy-start(f32[768]{0:T(1024)} %param.27) | copy-start | bytes 9220
  9.6 27.5 %copy-start.8 = (f32[768]{0:T(1024)S(1)}, f32[768]{0:T(1024)}, u32[]{:S(2)}) copy-start(f32[768]{0:T(1024)} %param.31) | copy-start | bytes 9220
  9.6 27.6 %copy-start.9 = (f32[768]{0:T(1024)S(1)}, f32[768]{0:T(1024)}, u32[]{:S(2)}) copy-start(f32[768]{0:T(1024)} %param.32) | copy-start | bytes 9220
  9.7 27.6 %copy-start.10 = (f32[768]{0:T(1024)S(1)}, f32[768]{0:T(1024)}, u32[]{:S(2)}) copy-start(f32[768]{0:T(1024)} %param.33) | copy-start | bytes 9220
  37.9 1.6 copy-start.2
  38.0 0.8 copy-start.3
  38.7 0.7 copy-start.4

commit v3 on v2

--- a/solution.py
+++ b/solution.py
@@ -1319,20 +1319,15 @@
     small_event(1)
     first_hop(1, 2)
     two_event(1)
-    line_start(1, 0)
     two_event(0)
-    line_start(0, 0)
-    line_start(1, 1)
-    line_start(0, 1)
     small_event(2)
     one_event(2)
     one_event(3)
     small_event(3)
     two_event(2)
     for k in range(3):
-        line_start(2, k)
-    line_start(1, 2)
-    line_start(0, 2)
+        for n in (1, 0, 2):
+            line_start(n, k)
     two_event(3)
     small_event(4)
     loads[10].wait()

time: 272 us -> 260 us (0.956)
  Pallas kernels: 257 us -> 246 us
    pallas_call x1, Pallas kernels: 104 us -> 95.8 us  [tail(): pl.pallas_call(tail_kernel, out_shape=[own(quarter, model), own(ff, model...]
where the time goes in v3:
time: 260 us; the launch traced here: 259 us
  Pallas kernels  246 us (95%)
  starting transfers between devices  6.2 us (2%)
  local copies, waits for them, and re-layouts  3.9 us (2%)
    pallas_call x1, Pallas kernels, tail(): pl.pallas_call(tail_kernel, out_shape=[own(quarter, model), own(ff, model...  95.8 us
    pallas_call x1, Pallas kernels, ffn_middle(): pl.pallas_call(partial(middle_kernel, share), out_shape=[shape(*x) for x...  89.9 us
    pallas_call x1, Pallas kernels, mix_backward(): pl.pallas_call(partial(mix_backward_kernel, slots, marks, taps), out_shap...  28.8 us
    pallas_call x1, Pallas kernels, mix_forward(): pl.pallas_call(partial(mix_forward_kernel, slots, marks, taps), out_shape...  26.4 us
    ppermute x3, starting transfers between devices, slice_body(): lax.ppermute(pack, 'heads', [(n, (n + i) % 4) for n in range(4)])  6.2 us
  transfers between devices with their start and end apart: 3, of which 1 were waited for; matrix products, arithmetic and copies ran while one was open for 0% of the time, Pallas kernels for 10%

profile of v3, /device:TPU:0, one launch (start us, length us, event | category | flops | bytes accessed | tf_op | source)
XLA Modules:
  0.0 259.0 jit_solution(13878883347726010135)
XLA Ops:
  0.6 0.0 copy-start
  0.7 0.9 copy-done
  1.6 0.8 dynamic_update_slice.6
  2.4 1.0 fusion.1.own0
  3.4 0.0 copy-start.1
  3.4 5.2 %collective-permute-start.2 = (bf16[224,768]{1,0:T(8,128)(2,1)S(1)}, bf16[224,768]{1,0:T(8,128)(2,1)S(1)}, u32[]{:S(2)}, u32[]{:S(2)}) collective-permute-start(bf16[224,768]{1,0:T(8,128)(2,1)S(1)} %fusion.1.own0), channel_id=1, source_target_pairs={{0,3},{1,0},{2,1},{3,2},{4,7},{5,4},{6,5},{7,6},{8,11},{9,8},{10,9... | collective-permute-start | bytes 1032200 | tf_op jit(solution)/shard_map/ppermute | solution.py:1969
  8.6 0.0 collective-permute-start.1
  8.6 1.0 collective-permute-start
  9.6 0.0 copy-start.5
  9.6 0.0 copy-start.6
  9.6 0.0 copy-start.7
  9.6 0.0 copy-start.8
  9.6 0.0 copy-start.9
  9.7 0.0 copy-start.10
  9.7 26.4 %mix_forward.1 = (bf16[576,3072]{1,0:T(8,128)(2,1)}, bf16[192,3072]{1,0:T(8,128)(2,1)}, bf16[192,3072]{1,0:T(8,128)(2,1)}, bf16[192,3072]{1,0:T(8,128)(2,1)}, f3...) custom-call(s32[3]{0:T(128)} %len_ref.5, ...), custom_call_target="tpu_custom_call" | custom-call | flops 20000000000 | bytes 30000000 | tf_op jit(solution)/shard_map/mix_forward/pallas_call | solution.py:673
  36.1 0.0 copy-done.1
  36.1 0.0 copy-done.5
  36.1 0.0 copy-done.6
  36.2 0.0 copy-done.7
  36.2 0.0 copy-done.8
  36.2 0.0 copy-done.9
  36.2 0.0 copy-done.10
  36.2 0.6 stack.27.vec_ref
  36.9 0.0 collective-permute-done.2.own3
  36.9 0.0 copy-start.2
  36.9 1.1 collective-permute-done.1.own2
  38.0 0.0 copy-start.3
  38.0 0.0 collective-permute-done.own1
  38.0 0.7 copy-done.3
  38.7 0.0 copy-start.4
  38.7 0.7 copy-done.4
  39.4 0.0 copy-done.2
  39.4 89.9 %middle.1 = (bf16[768,768]{1,0:T(8,128)(2,1)}, f32[768,768]{1,0:T(8,128)}, bf16[768,768]{1,0:T(8,128)(2,1)}, bf16[768,3072]{1,0:T(8,128)(2,1)}, bf16[768,3072]{1...) custom-call(bf16[192,3072]{1,0:T(8,128)(2,1)} %get-tuple-element.71., ...), custom_call_target="tpu_custom_call" | custom-call | tf_op jit(solution)/shard_map/middle/pallas_call | solution.py:1854
  129.3 28.8 %mix_backward.1 = (bf16[576,3072]{1,0:T(8,128)(2,1)}, f32[8,192]{1,0:T(8,128)}, f32[3,128]{1,0:T(4,128)}) custom-call(s32[3]{0:T(128)} %len_ref.5, bf16[192,3072]{1,0:T(8,128)(2,1)} %get-tuple-element.73.grad_ref, bf16[576,3072]{1,0:T(8,128)(2,1)} %get-tuple-element.74.qkv_ref, bf16[192,3072]{1,0:T(8,128)(2,1)} %get-tuple-element.75.first_ref, ...), custom_call_target="tpu_custom_call" | custom-call | flops 20000000000 | bytes 30000000 | tf_op jit(solution)/shard_map/mix_backward/pallas_call | solution.py:720
  158.2 95.8 %tail.1 = (f32[768,768]{1,0:T(8,128)}, f32[96,768]{1,0:T(8,128)}, f32[96,768]{1,0:T(8,128)}, f32[192,96]{1,0:T(8,128)}, f32[3,96,192]{2,1,0:T(8,128)}, /*index=5...) custom-call(s32[3]{0:T(128)} %len_ref.5, ...), custom_call_target="tpu_custom_call" | custom-call | tf_op jit(solution)/shard_map/tail/pallas_call | solution.py:1425
  254.0 4.8 %settle.1 = (bf16[768,768]{1,0:T(8,128)(2,1)}, f32[768,768]{1,0:T(8,128)}, f32[96,768]{1,0:T(8,128)}, f32[96,768]{1,0:T(8,128)}, f32[192,96]{1,0:T(8,128)}, /*in...) custom-call(bf16[768,768]{1,0:T(8,128)(2,1)} %get-tuple-element.72.r, ...), custom_call_target="tpu_custom_call" | custom-call | tf_op jit(solution)/shard_map/settle/pallas_call | solution.py:1917
  (8 shorter events, 0.0 us)
Async XLA Ops:
  0.6 1.0 copy-start
  3.4 32.7 %copy-start.1 = (bf16[224,768]{1,0:T(8,128)(2,1)}, bf16[224,768]{1,0:T(8,128)(2,1)S(1)}, u32[]{:S(2)}) copy-start(bf16[224,768]{1,0:T(8,128)(2,1)S(1)} %fusion.1.own0) | copy-start | bytes 1032196
  3.4 33.5 %collective-permute-start.2 = (bf16[224,768]{1,0:T(8,128)(2,1)S(1)}, bf16[224,768]{1,0:T(8,128)(2,1)S(1)}, u32[]{:S(2)}, u32[]{:S(2)}) collective-permute-start(bf16[224,768]{1,0:T(8,128)(2,1)S(1)} %fusion.1.own0), channel_id=1, source_target_pairs={{0,3},{1,0},{2,1},{3,2},{4,7},{5,4},{6,5},{7,6},{8,11},{9,8},{10,9... | collective-permute-start | bytes 1032200 | tf_op jit(solution)/shard_map/ppermute | solution.py:1969
  8.6 29.3 %collective-permute-start.1 = (bf16[224,768]{1,0:T(8,128)(2,1)S(1)}, bf16[224,768]{1,0:T(8,128)(2,1)S(1)}, u32[]{:S(2)}, u32[]{:S(2)}) collective-permute-start(bf16[224,768]{1,0:T(8,128)(2,1)S(1)} %fusion.1.own0), channel_id=1, source_target_pairs={{0,2},{1,3},{2,0},{3,1},{4,6},{5,7},{6,4},{7,5},{8,10},{9,11},{10,... | collective-permute-start | bytes 1032200 | tf_op jit(solution)/shard_map/ppermute | solution.py:1969
  8.6 29.3 %collective-permute-start = (bf16[224,768]{1,0:T(8,128)(2,1)S(1)}, bf16[224,768]{1,0:T(8,128)(2,1)S(1)}, u32[]{:S(2)}, u32[]{:S(2)}) collective-permute-start(bf16[224,768]{1,0:T(8,128)(2,1)S(1)} %fusion.1.own0), channel_id=1, source_target_pairs={{0,1},{1,2},{2,3},{3,0},{4,5},{5,6},{6,7},{7,4},{8,9},{9,10},{10,1... | collective-permute-start | bytes 1032200 | tf_op jit(solution)/shard_map/ppermute | solution.py:1969
  9.6 26.5 %copy-start.5 = (f32[768]{0:T(1024)S(1)}, f32[768]{0:T(1024)}, u32[]{:S(2)}) copy-start(f32[768]{0:T(1024)} %param.25) | copy-start | bytes 9220
  9.6 26.5 %copy-start.6 = (f32[768]{0:T(1024)S(1)}, f32[768]{0:T(1024)}, u32[]{:S(2)}) copy-start(f32[768]{0:T(1024)} %param.26) | copy-start | bytes 9220
  9.6 26.5 %copy-start.7 = (f32[768]{0:T(1024)S(1)}, f32[768]{0:T(1024)}, u32[]{:S(2)}) copy-start(f32[768]{0:T(1024)} %param.27) | copy-start | bytes 9220
  9.6 26.5 %copy-start.8 = (f32[768]{0:T(1024)S(1)}, f32[768]{0:T(1024)}, u32[]{:S(2)}) copy-start(f32[768]{0:T(1024)} %param.31) | copy-start | bytes 9220
  9.6 26.6 %copy-start.9 = (f32[768]{0:T(1024)S(1)}, f32[768]{0:T(1024)}, u32[]{:S(2)}) copy-start(f32[768]{0:T(1024)} %param.32) | copy-start | bytes 9220
  9.7 26.6 %copy-start.10 = (f32[768]{0:T(1024)S(1)}, f32[768]{0:T(1024)}, u32[]{:S(2)}) copy-start(f32[768]{0:T(1024)} %param.33) | copy-start | bytes 9220
  36.9 2.5 copy-start.2
  38.0 0.7 copy-start.3
  38.7 0.7 copy-start.4
